TPU v7x, 256 devices: a whole 4x4x8 slice. The times are simulated.
256 devices in a mesh: gx: 2 (over x_hi), gy: 2 (over core), gz: 64 (over z, y, x_lo).
Axes of the slice: x: 4 (x_hi: 2, x_lo: 2; x = x_hi * 2 + x_lo), y: 4, z: 8, core: 2. Of those that a mesh axis runs over, the one named last changes fastest.
Arguments:
- state: float32 [24, 32, 128, 512], P(None, 'gx', ('gy', 'gz')), may hold values from -6 to 6
- base: float32 [24, 32, 128, 512], P(None, 'gx', ('gy', 'gz')), may hold values from -0.6 to 0.6
- accum: float32 [24, 32, 128, 512], P(None, 'gx', ('gy', 'gz')), may hold values from -0.3 to 0.3
- owner: int32 [64], replicated, may hold values from 0 to 63, each once
Outputs:
- next_section: float32 [24, 32, 128, 512], P(None, 'gx', ('gy', 'gz'))
- accum_out: float32 [24, 32, 128, 512], P(None, 'gx', ('gy', 'gz'))
Inputs may be any that keep to these rules, and one draw needn't show every extreme that they name: owner names every index of gz once.
All inputs are finite; a program needn't handle non-finite values.
Results may differ from a plain program's by a relative error of at most 0.00002.
Values sent between devices are 32-bit elements; how exact they have to be, the bound alone decides.
A program may use at most 192 MiB of HBM per device.

v0:
```python
import jax
import jax.numpy as jnp
from jax import lax
from jax.sharding import PartitionSpec as P

BLOCK = 16


DAMPING_STRENGTH = 1.0
SPACING = 1.0
TIME_STEP = 0.25
SECTION_SHIFT = 0.5
SECTION_WEIGHT = 1.0 / 3.0


def extended_2(block, sides, width):
    for axis, dim in sides:
        count = lax.axis_size(axis)
        forward = [(i, i + 1) for i in range(count - 1)]
        forward.append((count - 1, 0))
        backward = [(target, source) for source, target in forward]
        low = lax.ppermute(
            lax.slice_in_dim(block, block.shape[dim] - width, None, axis=dim), axis, forward
        )
        high = lax.ppermute(lax.slice_in_dim(block, 0, width, axis=dim), axis, backward)
        block = jnp.concatenate([low, block, high], axis=dim)
    return block


def axis_terms(extended, dimension):
    length = extended.shape[dimension] - 6
    values = [
        lax.slice_in_dim(extended, 3 + offset, 3 + offset + length, axis=dimension)
        for offset in range(-3, 4)
    ]
    laplace = (-values[1] + 16.0 * values[2] - 30.0 * values[3] + 16.0 * values[4] - values[5]) / (
        12.0 * SPACING * SPACING
    )
    damping = (
        values[0]
        - 6.0 * values[1]
        + 15.0 * values[2]
        - 20.0 * values[3]
        + 15.0 * values[4]
        - 6.0 * values[5]
        + values[6]
    ) * (DAMPING_STRENGTH / (64.0 * SPACING))
    return (laplace, damping)


def rates_from(centre, laplace, damping):
    halves = centre.shape[0] // 2
    metric = centre[:halves]
    curvature = centre[halves:]
    lapse_value = 1.0 + 0.25 * jnp.tanh(metric[0])
    trace_value = jnp.mean(curvature, axis=0)
    metric_rate = -2.0 * lapse_value * curvature + damping[:halves]
    curvature_rate = (
        -0.5 * lapse_value * laplace[:halves]
        + lapse_value * trace_value * curvature
        + damping[halves:]
    )
    return jnp.concatenate([metric_rate, curvature_rate], axis=0)


def layers_ghosts(cells):
    return extended_2(cells, (("gx", 1),), 3)


def rows_ghosts(cells):
    return extended_2(cells, (("gy", 2),), 3)


def local(state, base, accum, owner):
    fields = state.shape[0]
    thickness = state.shape[1]
    side_y = BLOCK
    side_z = 2 * BLOCK
    columns = lax.axis_size("gz")
    labels = jnp.arange(columns, dtype=jnp.int32)
    matches = owner[:, None] == labels[None, :]
    column_of = jnp.sum(jnp.where(matches, labels[:, None], 0), axis=0)
    below = jnp.take(owner, (column_of + columns - 1) % columns)
    above = jnp.take(owner, (column_of + 1) % columns)
    tile_cells = state.reshape(fields, thickness, side_y, side_z)
    row_count = tile_cells.shape[1]
    width = tile_cells.shape[2]
    depth = tile_cells.shape[3]
    low_face = tile_cells[:, :, :, :3].reshape(-1)
    high_face = tile_cells[:, :, :, depth - 3 :].reshape(-1)
    total = low_face.shape[0]
    piece = -(-total // columns)
    padded_len = piece * columns
    faces = jnp.stack([low_face, high_face])
    outgoing = faces.reshape(2, columns, piece).transpose(1, 0, 2)
    spread = lax.all_to_all(outgoing, "gz", split_axis=0, concat_axis=0, tiled=True)
    forwarded = jnp.stack([spread[below, 1], spread[above, 0]], axis=1)
    arrived = lax.all_to_all(forwarded, "gz", split_axis=0, concat_axis=0, tiled=True)
    ghosts = arrived.transpose(1, 0, 2).reshape(2, padded_len)
    ghost_shape = (fields, row_count, width, 3)
    extended = [
        layers_ghosts(tile_cells),
        rows_ghosts(tile_cells),
        jnp.concatenate(
            [ghosts[0].reshape(ghost_shape), tile_cells, ghosts[1].reshape(ghost_shape)], axis=3
        ),
    ]
    laplace = 0.0
    damping = 0.0
    for position, dimension in enumerate((1, 2, 3)):
        laplace_part, damping_part = axis_terms(extended[position], dimension)
        laplace = laplace + laplace_part
        damping = damping + damping_part
    rate_values = rates_from(tile_cells, laplace, damping).reshape(state.shape)
    next_section = base + SECTION_SHIFT * TIME_STEP * rate_values
    accum_out = accum + SECTION_WEIGHT * TIME_STEP * rate_values
    return (next_section, accum_out)


def solution(mesh):
    return jax.shard_map(
        local,
        mesh=mesh,
        in_specs=(
            P(None, "gx", ("gy", "gz"), None),
            P(None, "gx", ("gy", "gz"), None),
            P(None, "gx", ("gy", "gz"), None),
            P(),
        ),
        out_specs=(P(None, "gx", ("gy", "gz"), None), P(None, "gx", ("gy", "gz"), None)),
        check_vma=False,
    )
```

profile of v0, /device:TPU:1, one launch (start us, length us, event | category | flops | bytes accessed | tf_op | source)
XLA Modules:
  0.0 159.0 jit_solution(2464243631213242564)
XLA Ops:
  0.6 3.9 %reduce.3 = f32[24,16,512]{2,1,0:T(8,128)} reduce(f32[24,16,1,512]{3,2,1,0:T(1,128)} %param.6, f32[]{:T(128)} %constant.108), dimensions={2}, to_apply=%param.6.reduce_sub_computation | reduce | bytes 1572868 | tf_op args[0]
  4.6 1.9 %reshape.86 = f32[24,16,16,32]{3,2,1,0:T(8,128)S(1)} reshape(f32[24,16,512]{2,1,0:T(8,128)} %reduce.3) | data formatting | bytes 1572864 | tf_op jit(solution)/shard_map/reshape | solution.py:85
  6.4 3.7 %fusion.43 = (f32[24,16,16,3]{3,2,1,0:T(8,128)}, f32[24,16,16,3]{3,2,1,0:T(8,128)}) fusion(f32[24,16,16,32]{3,2,1,0:T(8,128)S(1)} %reshape.86), kind=kLoop, calls=%fused_computation.110 | loop fusion | bytes 294912 | tf_op jit(solution)/shard_map/slice | solution.py:89
  10.1 4.0 %stack.22 = f32[1,64,288]{2,0,1:T(1,128)S(1)} reshape(f32[24,16,16,3]{3,2,1,0:T(8,128)} %get-tuple-element.35) | data formatting | bytes 147456 | tf_op jit(solution)/shard_map/stack | solution.py:94
  14.2 4.0 %stack.23 = f32[1,64,288]{2,0,1:T(1,128)S(1)} reshape(f32[24,16,16,3]{3,2,1,0:T(8,128)} %get-tuple-element.36) | data formatting | bytes 147456 | tf_op jit(solution)/shard_map/stack | solution.py:94
  18.2 0.9 maximum_bitcast_fusion
  19.1 13.6 %all-to-all-start = ((f32[64,2,288]{2,1,0:T(2,128)}), f32[64,2,288]{2,1,0:T(2,128)S(1)}, u32[]{:S(2)}, u32[]{:S(2)}) async-start(f32[64,2,288]{2,1,0:T(2,128)} %maximum_bitcast_fusion), calls=%async_computation | async-start | bytes 393216 | tf_op jit(solution)/shard_map/all_to_all | solution.py:96
  32.7 0.4 fusion.42
  33.1 0.0 copy-start.4
  33.1 0.0 copy-start
  33.1 0.9 copy.29
  34.0 1.0 collective-permute-start.2
  34.9 1.1 fusion.41
  36.1 2.5 %collective-permute-start = (f32[24,3,16,32]{3,2,1,0:T(8,128)}, f32[24,3,16,32]{3,2,1,0:T(8,128)}, u32[]{:S(2)}, u32[]{:S(2)}) collective-permute-start(f32[24,3,16,32]{3,2,1,0:T(8,128)} %get-tuple-element.31), channel_id=1, source_target_pairs={{0,128},{128,0},{1,129},{129,1},{2,130},{130,2},{3,131},{131,3},{4... | collective-permute-start | bytes 442376 | tf_op jit(solution)/shard_map/ppermute | solution.py:22
  38.5 0.5 collective-permute-start.1
  39.1 0.9 copy.31
  39.9 0.6 collective-permute-start.3
  40.5 0.0 copy-done.4
  40.5 1.9 %slice_reduce_fusion = (f32[16,512]{1,0:T(8,128)S(1)}, f32[12,16,512]{2,1,0:T(8,128)}) fusion(f32[24,16,1,512]{3,2,1,0:T(1,128)S(1)} %copy-done.4), kind=kLoop, calls=%fused_computation.68 | loop fusion | flops 90112 | bytes 819200 | tf_op jit(solution)/shard_map/reduce_sum | solution.py:56
  42.4 0.0 copy-done
  42.4 0.1 select_reduce_fusion
  42.5 0.8 gather_fusion.2
  43.3 0.8 gather_fusion.3
  44.1 0.8 div.22
  44.8 0.9 add_reduce_fusion
  45.7 0.7 add.128
  46.4 2.6 %slice.122 = f32[12,16,16,32]{3,2,1,0:T(8,128)} reshape(f32[12,16,512]{2,1,0:T(8,128)} %get-tuple-element.8) | data formatting | bytes 786432 | tf_op jit(solution)/shard_map/slice | solution.py:54
  49.0 0.0 all-to-all-done
  49.0 0.8 gather_fusion
  49.8 0.8 gather_fusion.1
  50.6 0.8 copy.35
  51.5 11.1 %all-to-all-start.1 = ((f32[64,2,288]{2,1,0:T(2,128)}), f32[64,2,288]{2,1,0:T(2,128)S(1)}, u32[]{:S(2)}, u32[]{:S(2)}) async-start(f32[64,2,288]{2,1,0:T(2,128)} %copy.35), calls=%async_computation.1 | async-start | bytes 393216 | tf_op jit(solution)/shard_map/all_to_all | solution.py:98
  62.6 1.7 %broadcast_multiply_fusion.3 = (f32[16,16,32]{2,1,0:T(8,128)S(1)}, f32[16,16,32]{2,1,0:T(8,128)}, f32[16,16,32]{2,1,0:T(8,128)}) fusion(f32[16,16,32]{2,1,0:T(8,128)} %add.128, f32[16,16,32]{2,1,0:T(8,128)} %div.22), kind=kLoop, calls=%fused_computation.75 | loop fusion | flops 24576 | bytes 163840 | tf_op jit(solution)/shard_map/mul | solution.py:57
  64.4 0.0 collective-permute-done.2
  64.4 2.2 %copy.30 = f32[24,16,3,32]{3,2,1,0:T(4,128)} copy(f32[24,16,3,32]{3,1,2,0:T(8,128)} %collective-permute-done.2) | data formatting | bytes 294912 | tf_op jit(solution)/shard_map/ppermute | solution.py:22
  66.6 0.0 collective-permute-done
  66.6 1.9 %constant_dynamic-update-slice_fusion.1 = f32[24,19,16,32]{3,2,1,0:T(8,128)} fusion(f32[24,3,16,32]{3,2,1,0:T(8,128)} %collective-permute-done), kind=kLoop, calls=%fused_computation.81 | loop fusion | bytes 737280
  68.6 4.4 %all-to-all-done.1 = f32[64,2,288]{2,1,0:T(2,128)S(1)} async-done(((f32[64,2,288]{2,1,0:T(2,128)}), f32[64,2,288]{2,1,0:T(2,128)S(1)}, u32[]{:S(2)}, u32[]{:S(2)}) %all-to-all-start.1) | async-done | bytes 147488 | tf_op jit(solution)/shard_map/all_to_all | solution.py:98
  73.0 1.1 slice_reduce_fusion.3
  74.1 4.9 %reshape_squeeze.6 = f32[24,16,16,3]{3,2,1,0:T(8,128)} reshape(f32[64,288]{1,0:T(8,128)} %get-tuple-element.9) | data formatting | bytes 147456 | tf_op jit(solution)/shard_map/reshape;squeeze | solution.py:105
  79.0 12.6 %broadcast_multiply_fusion = (f32[24,16,16,32]{3,2,1,0:T(8,128)}, f32[24,16,16,32]{3,2,1,0:T(8,128)}, f32[24,16,16,32]{3,2,1,0:T(8,128)}, f32[24,16,16,32]{3,2,1...) fusion(f32[24,16,16,32]{3,2,1,0:T(8,128)S(1)} %reshape.86, ...), kind=kLoop, calls=%fused_computation.62 | loop fusion | flops 1966078 | bytes 26738688 | tf_op jit(solution)/shard_map/mul | solution.py:36
  91.6 0.0 collective-permute-done.1
  91.6 1.1 constant_dynamic-update-slice_fusion.2
  92.7 0.0 copy-start.1
  92.7 0.0 copy-start.6
  92.7 3.6 %fusion.40 = (f32[24,16,16,32]{3,2,1,0:T(8,128)}, f32[24,16,16,32]{3,2,1,0:T(8,128)}) fusion(f32[24,19,16,32]{3,2,1,0:T(8,128)S(1)} %constant_dynamic-update-slice_fusion.2), kind=kLoop, calls=%fused_computation.107 | loop fusion | bytes 3145728 | tf_op jit(solution)/shard_map/slice | solution.py:33
  96.3 0.2 copy-done.1
  96.5 0.0 copy-done.6
  96.5 4.8 %reshape_squeeze.7 = f32[24,16,16,3]{3,2,1,0:T(8,128)} reshape(f32[64,288]{1,0:T(8,128)S(1)} %copy-done.6) | data formatting | bytes 147456 | tf_op jit(solution)/shard_map/reshape;squeeze | solution.py:105
  101.3 0.0 collective-permute-done.3
  101.3 2.3 %copy_dynamic-update-slice_fusion = f32[24,16,19,32]{3,2,1,0:T(8,128)} fusion(f32[24,16,19,32]{3,2,1,0:T(8,128)} %get-tuple-element.28, f32[24,16,3,32]{3,1,2,0:T(8,128)} %collective-permute-done.3), kind=kLoop, calls=%fused_computation.66 | loop fusion | bytes 1376256 | tf_op jit(solution)/shard_map/concatenate | solution.py:26
  103.7 7.4 %fusion.39 = (f32[24,16,16,32]{3,2,1,0:T(8,128)}, f32[24,16,16,32]{3,2,1,0:T(8,128)}) fusion(f32[24,16,19,32]{3,2,1,0:T(8,128)} %copy_dynamic-update-slice_fusion), kind=kLoop, calls=%fused_computation.106 | loop fusion | bytes 3145728 | tf_op jit(solution)/shard_map/slice | solution.py:33
  111.1 0.0 copy-done.2
  111.1 2.1 %multiply_add_fusion.1 = f32[24,16,16,32]{3,2,1,0:T(8,128)} fusion(f32[24,19,16,32]{3,2,1,0:T(8,128)S(1)} %copy-done.2), kind=kLoop, calls=%fused_computation.39 | loop fusion | flops 589824 | bytes 2359296 | tf_op jit(solution)/shard_map/add | solution.py:36
  113.2 0.9 copy-done.3
  114.1 21.6 %fusion.10 = (f32[24,16,16,32]{3,2,1,0:T(8,128)}, f32[24,16,16,32]{3,2,1,0:T(8,128)}, f32[24,16,16,32]{3,2,1,0:T(8,128)}) fusion(f32[24,16,16,32]{3,2,1,0:T(8,128)S(1)} %reshape.86, f32[24,16,3,32]{3,2,1,0:T(4,128)} %copy.30, f32[24,16,16,3]{3,2,1,0:T(8,128)} %reshape_squeeze.7, f32[24,16,19,32]{3,2,1,0:T(8,128)} %copy_dynamic-update-slice_fusion, ...), kind=kLoop, calls=%fused_computation.18 | loop fusion | flops 8454144 | bytes 10518528 | tf_op jit(solution)/shard_map/add | solution.py:113
  135.8 8.9 %slice_add_fusion.2 = (f32[12,16,16,32]{3,2,1,0:T(8,128)S(1)}, f32[12,16,16,32]{3,2,1,0:T(8,128)S(1)}) fusion(f32[24,16,16,32]{3,2,1,0:T(8,128)} %get-tuple-element.11, f32[12,16,16,32]{3,2,1,0:T(8,128)} %slice.122, f32[16,16,32]{2,1,0:T(8,128)S(1)} %get-tuple-element.37, f32[16,16,32]{2,1,0:T(8,128)S(1)} %copy-done.5, ...), kind=kLoop, calls=%fused_computation.61 | loop fusion | flops 2162688 | bytes 6389760 | tf_op jit(solution)/shard_map/add | solution.py:57
  144.7 2.4 %fusion.20 = (f32[24,16,16,32]{3,2,1,0:T(8,128)S(1)}, f32[24,16,16,32]{3,2,1,0:T(8,128)}) fusion(f32[12,16,16,32]{3,2,1,0:T(8,128)S(1)} %get-tuple-element.17, f32[12,16,16,32]{3,2,1,0:T(8,128)S(1)} %get-tuple-element.16), kind=kLoop, calls=%fused_computation.40 | loop fusion | flops 589824 | bytes 2359296 | tf_op jit(solution)/shard_map/mul | solution.py:116
  147.1 3.4 %mul.205 = f32[24,16,1,512]{3,1,0,2:T(8,128)} reshape(f32[24,16,16,32]{3,2,1,0:T(8,128)} %get-tuple-element.23) | data formatting | bytes 1572864 | tf_op jit(solution)/shard_map/mul | solution.py:115
  150.5 1.5 copy_add_fusion.1
  152.0 1.7 %copy.38 = f32[24,16,1,512]{3,2,1,0:T(1,128)} copy(f32[24,16,1,512]{3,1,0,2:T(8,128)S(1)} %copy_add_fusion.1) | data formatting | bytes 1572864
  153.7 2.1 %mul.207 = f32[24,16,1,512]{3,1,0,2:T(8,128)} reshape(f32[24,16,16,32]{3,2,1,0:T(8,128)S(1)} %get-tuple-element.22) | data formatting | bytes 1572864 | tf_op jit(solution)/shard_map/mul | solution.py:116
  155.8 1.5 copy_add_fusion
  157.3 1.7 %copy.39 = f32[24,16,1,512]{3,2,1,0:T(1,128)} copy(f32[24,16,1,512]{3,1,0,2:T(8,128)S(1)} %copy_add_fusion) | data formatting | bytes 1572864
  (10 shorter events, 0.1 us)
Async XLA Ops:
  19.1 29.9 %all-to-all-start = ((f32[64,2,288]{2,1,0:T(2,128)}), f32[64,2,288]{2,1,0:T(2,128)S(1)}, u32[]{:S(2)}, u32[]{:S(2)}) async-start(f32[64,2,288]{2,1,0:T(2,128)} %maximum_bitcast_fusion), calls=%async_computation | async-start | bytes 393216 | tf_op jit(solution)/shard_map/all_to_all | solution.py:96
  33.1 7.4 %copy-start.4 = (f32[24,16,1,512]{3,2,1,0:T(1,128)S(1)}, f32[24,16,1,512]{3,2,1,0:T(1,128)}, u32[]{:S(2)}) copy-start(f32[24,16,1,512]{3,2,1,0:T(1,128)} %param.6) | copy-start | bytes 2359300
  33.1 9.3 %copy-start = (s32[64]{0:T(128)S(1)}, s32[64]{0:T(128)}, u32[]{:S(2)}) copy-start(s32[64]{0:T(128)} %param.9) | copy-start | bytes 772
  34.0 30.4 %collective-permute-start.2 = (f32[24,16,3,32]{3,1,2,0:T(8,128)}, f32[24,16,3,32]{3,1,2,0:T(8,128)}, u32[]{:S(2)}, u32[]{:S(2)}) collective-permute-start(f32[24,16,3,32]{3,1,2,0:T(8,128)} %copy.29), channel_id=1, source_target_pairs={{0,64},{64,0},{1,65},{65,1},{2,66},{66,2},{3,67},{67,3},{4,68},{68... | collective-permute-start | bytes 442376 | tf_op jit(solution)/shard_map/ppermute | solution.py:22
  36.1 30.5 %collective-permute-start = (f32[24,3,16,32]{3,2,1,0:T(8,128)}, f32[24,3,16,32]{3,2,1,0:T(8,128)}, u32[]{:S(2)}, u32[]{:S(2)}) collective-permute-start(f32[24,3,16,32]{3,2,1,0:T(8,128)} %get-tuple-element.31), channel_id=1, source_target_pairs={{0,128},{128,0},{1,129},{129,1},{2,130},{130,2},{3,131},{131,3},{4... | collective-permute-start | bytes 442376 | tf_op jit(solution)/shard_map/ppermute | solution.py:22
  38.5 53.0 %collective-permute-start.1 = (f32[24,3,16,32]{3,2,1,0:T(8,128)}, f32[24,3,16,32]{3,2,1,0:T(8,128)}, u32[]{:S(2)}, u32[]{:S(2)}) collective-permute-start(f32[24,3,16,32]{3,2,1,0:T(8,128)} %get-tuple-element.32), channel_id=1, source_target_pairs={{128,0},{0,128},{129,1},{1,129},{130,2},{2,130},{131,3},{3,131},{1... | collective-permute-start | bytes 442376 | tf_op jit(solution)/shard_map/ppermute | solution.py:25
  39.9 61.4 %collective-permute-start.3 = (f32[24,16,3,32]{3,1,2,0:T(8,128)}, f32[24,16,3,32]{3,1,2,0:T(8,128)}, u32[]{:S(2)}, u32[]{:S(2)}) collective-permute-start(f32[24,16,3,32]{3,1,2,0:T(8,128)} %copy.31), channel_id=1, source_target_pairs={{64,0},{0,64},{65,1},{1,65},{66,2},{2,66},{67,3},{3,67},{68,4},{4,... | collective-permute-start | bytes 442376 | tf_op jit(solution)/shard_map/ppermute | solution.py:25
  51.5 21.5 %all-to-all-start.1 = ((f32[64,2,288]{2,1,0:T(2,128)}), f32[64,2,288]{2,1,0:T(2,128)S(1)}, u32[]{:S(2)}, u32[]{:S(2)}) async-start(f32[64,2,288]{2,1,0:T(2,128)} %copy.35), calls=%async_computation.1 | async-start | bytes 393216 | tf_op jit(solution)/shard_map/all_to_all | solution.py:98
  92.7 3.8 %copy-start.1 = (f32[24,19,16,32]{3,2,1,0:T(8,128)}, f32[24,19,16,32]{3,2,1,0:T(8,128)S(1)}, u32[]{:S(2)}) copy-start(f32[24,19,16,32]{3,2,1,0:T(8,128)S(1)} %constant_dynamic-update-slice_fusion.2) | copy-start | bytes 2801668
  92.7 3.8 %copy-start.6 = (f32[64,288]{1,0:T(8,128)S(1)}, f32[64,288]{1,0:T(8,128)}, u32[]{:S(2)}) copy-start(f32[64,288]{1,0:T(8,128)} %get-tuple-element.10) | copy-start | bytes 221188
  103.7 7.4 %copy-start.2 = (f32[24,19,16,32]{3,2,1,0:T(8,128)S(1)}, f32[24,19,16,32]{3,2,1,0:T(8,128)}, u32[]{:S(2)}) copy-start(f32[24,19,16,32]{3,2,1,0:T(8,128)} %get-tuple-element.30) | copy-start | bytes 2801668
  111.1 3.0 %copy-start.3 = (f32[24,16,16,3]{3,2,1,0:T(8,128)S(1)}, f32[24,16,16,3]{3,2,1,0:T(8,128)}, u32[]{:S(2)}) copy-start(f32[24,16,16,3]{3,2,1,0:T(8,128)} %reshape_squeeze.6) | copy-start | bytes 221188
  114.1 21.6 %copy-start.5 = (f32[16,16,32]{2,1,0:T(8,128)S(1)}, f32[16,16,32]{2,1,0:T(8,128)}, u32[]{:S(2)}) copy-start(f32[16,16,32]{2,1,0:T(8,128)} %get-tuple-element.38) | copy-start | bytes 98308
where the time goes:
time: 160 us; the launch traced here: 159 us
  local copies, waits for them, and re-layouts  64.5 us (40%)
  other arithmetic  60.1 us (38%)
  starting transfers between devices  29.2 us (18%)
  waiting for transfers between devices  4.42 us (3%)
    add x1, other arithmetic, local(): damping = damping + damping_part  21.6 us
    all_to_all x1, starting transfers between devices, local(): lax.all_to_all(outgoing, 'gz', split_axis=0, concat_axis=0, tiled=True)  13.6 us
    mul x1, other arithmetic, axis_terms(): 30.0 * values[3]  12.6 us
    all_to_all x1, starting transfers between devices, local(): lax.all_to_all(forwarded, 'gz', split_axis=0, concat_axis=0, tiled=True)  11.1 us
    slice x2, local copies, waits for them, and re-layouts, axis_terms(): lax.slice_in_dim(extended, 3 + offset, 3 + offset + length, axis=dimension)  11 us
    add x1, other arithmetic, rates_from(): metric_rate = -2.0 * lapse_value * curvature + damping[:halves]  8.9 us
    another operation x2, local copies, waits for them, and re-layouts, local(): faces = jnp.stack([low_face, high_face])  8.07 us
    unnamed x17, local copies, waits for them, and re-layouts  6.52 us
  transfers between devices with their start and end apart: 6, of which 1 were waited for; matrix products, arithmetic and copies ran while one was open for 30% of the time, Pallas kernels for 0%

commit v1 on v0

v1 whole, which is shorter than its diff:
```python
import functools

import jax
import jax.numpy as jnp
from jax import lax
from jax.experimental import pallas as pl
from jax.experimental.pallas import tpu as pltpu
from jax.sharding import PartitionSpec as P

MESH = pl.DeviceIdType.MESH
FIELDS, HALF = 24, 12
LANES = 128
C1 = 0.5 * 0.25
C2 = 0.25 / 3.0
DAMP = (-20.0 / 64.0, 15.0 / 64.0, -6.0 / 64.0, 1.0 / 64.0)
LAP = (-30.0 / 12.0, 16.0 / 12.0, -1.0 / 12.0)
MIDS = 40


def lane_iota(rows=8):
    return lax.broadcasted_iota(jnp.int32, (rows, LANES), 1)


def roll(v, s):
    s %= LANES
    return v if s == 0 else pltpu.roll(v, s, axis=1)


def mid_of(w, i):
    return lax.rem(i + 3 * w, 8)


def kernel_a(state, base, accum, owner, q1, q2, gb, lapse_out,
             xp, sy, bs, ac, rt, lap, mb, rb, fb, xs, xr, tabv, tab,
             s_in, s_tab, s_out, s_y, r_y, s_x, r_x, s_1, r_1, s_2, r_2, s_self):
    gx, gy, me = lax.axis_index("gx"), lax.axis_index("gy"), lax.axis_index("gz")
    z, w = me // 8, lax.rem(me, 8)
    mine = lax.rem(z + 40 - 3 * w - 4 * gy, 8)
    is_mid = mine < 5
    my_g = w * 5 + mine

    load_state = pltpu.make_async_copy(state, xp.at[:, pl.ds(16, 64)], s_in.at[0])
    load_base = pltpu.make_async_copy(base, bs, s_in.at[1])
    load_accum = pltpu.make_async_copy(accum, ac, s_in.at[2])
    load_state.start()
    load_base.start()
    load_accum.start()

    barrier = pltpu.get_barrier_semaphore()

    @pl.loop(1, 64)
    def _(k):
        pl.semaphore_signal(barrier, inc=1, device_id={"gz": lax.rem(me + k, 64)}, device_id_type=MESH)

    pl.semaphore_signal(barrier, inc=1, device_id={"gy": 1 - gy}, device_id_type=MESH)
    pl.semaphore_signal(barrier, inc=1, device_id={"gx": 1 - gx}, device_id_type=MESH)

    lanes = lane_iota()
    below = jnp.zeros((8, LANES), jnp.int32)
    above = jnp.zeros((8, LANES), jnp.int32)
    for c in range(64):
        hit = lanes == owner[c]
        below = jnp.where(hit, owner[(c + 63) % 64], below)
        above = jnp.where(hit, owner[(c + 1) % 64], above)
    tabv[0] = below
    tabv[1] = above
    load_tab = pltpu.make_async_copy(tabv, tab, s_tab)

    b = lanes % 32
    u = (lanes + 3) % 32
    load_state.wait()
    load_tab.start()

    def tile(f, xg, q):
        return xp[f, pl.ds(16 + xg * 32 + q, 8, stride=4), :]

    @pl.loop(0, 8)
    def _(g):
        for p in range(5):
            acc = jnp.zeros((8, LANES), jnp.float32)
            for r in range(5 if p < 4 else 4):
                n = p * 5 + r
                v = tile(g * 3 + n // 8, (n % 8) // 4, n % 4)
                x = jnp.where(b < 3, roll(v, 32), roll(v, 96))
                window = (u + 32 - 6 * r) % 32 < 6
                acc = jnp.where(window, roll(x, 6 * r), acc)
            mb[g * 5 + p] = acc

    first = lax.broadcasted_iota(jnp.int32, (8, LANES), 0) < 4
    for f in range(0, FIELDS, 2):
        lo0, lo1 = xp[f, pl.ds(24, 8), :], xp[f + 1, pl.ds(24, 8), :]
        hi0, hi1 = xp[f, pl.ds(64, 8), :], xp[f + 1, pl.ds(64, 8), :]
        xs[0, f // 2] = jnp.where(first, lo0, pltpu.roll(lo1, 4, axis=0))
        xs[1, f // 2] = jnp.where(first, pltpu.roll(hi0, 4, axis=0), hi1)

    pl.semaphore_wait(barrier, 65)

    def send_1(k):
        dw, i = k // 5, lax.rem(k + z, 5)
        ow = lax.rem(w + dw, 8)
        oz = lax.rem(i + 3 * ow + 4 * gy, 8)
        peer = oz * 8 + ow
        return peer, ow * 5 + i

    @pl.loop(0, MIDS)
    def _(k):
        peer, g = send_1(k)

        @pl.when(peer != me)
        def _():
            pltpu.make_async_remote_copy(
                mb.at[g], rb.at[me], s_1, r_1, device_id={"gz": peer}, device_id_type=MESH).start()

    send_y = pltpu.make_async_remote_copy(
        xp.at[:, pl.ds(16, 64)], sy, s_y, r_y, device_id={"gy": 1 - gy}, device_id_type=MESH)
    send_y.start()
    send_x = [
        pltpu.make_async_remote_copy(
            xp.at[:, pl.ds(16, 8)], xp.at[:, pl.ds(80, 8)], s_x.at[0], r_x.at[0],
            device_id={"gx": 1 - gx}, device_id_type=MESH),
        pltpu.make_async_remote_copy(
            xp.at[:, pl.ds(72, 8)], xp.at[:, pl.ds(8, 8)], s_x.at[1], r_x.at[1],
            device_id={"gx": 1 - gx}, device_id_type=MESH),
        pltpu.make_async_remote_copy(
            xs, xr, s_x.at[2], r_x.at[2], device_id={"gx": 1 - gx}, device_id_type=MESH),
    ]
    for s in send_x:
        s.start()

    @pl.when(is_mid)
    def _():
        rb[me] = mb[my_g]

    load_tab.wait()
    send_y.wait_recv()

    for t in range(8):
        xg, q = t // 4, t % 4
        lap[t] = 1.0 + 0.25 * jnp.tanh(tile(0, xg, q))
        total = tile(12, xg, q)
        for f in range(13, 24):
            total = total + tile(f, xg, q)
        lap[8 + t] = lap[t] * (total * (1.0 / 12.0))

    low = [b >= k for k in (1, 2, 3)]
    high = [b < 32 - k for k in (1, 2, 3)]
    left = [lanes >= 32 * k for k in (1, 2, 3)]
    right = [lanes < 128 - 32 * k for k in (1, 2, 3)]

    def plane(f, xg):
        values = [sy[f, pl.ds(xg * 32 + 3, 8, stride=4), :]]
        values += [tile(f, xg, q) for q in range(4)]
        values += [sy[f, pl.ds(xg * 32, 8, stride=4), :]]
        turned = [[v] + [roll(v, 32 * j) for j in (1, 2, 3)] for v in values]
        sums = []
        for q in range(4):
            v = values[q + 1]
            three = []
            for k in (1, 2, 3):
                plus = jnp.where(right[k - 1], turned[q + 1][4 - k], turned[q + 2][4 - k])
                minus = jnp.where(left[k - 1], turned[q + 1][k], turned[q][k])
                up = jnp.where(high[k - 1], roll(v, -k), 0.0)
                down = jnp.where(low[k - 1], roll(v, k), 0.0)
                three.append((plus + minus) + (up + down))
            sums.append((v, three))
        return sums

    @pl.loop(0, HALF)
    def _(f):
        for xg in range(2):
            us, vs = plane(f, xg), plane(f + HALF, xg)
            for q in range(4):
                t = xg * 4 + q
                lapse, drag = lap[t], lap[8 + t]
                uv, (u1, u2, u3) = us[q]
                vv, (v1, v2, v3) = vs[q]
                damp_u = (2 * DAMP[0]) * uv + DAMP[1] * u1 + DAMP[2] * u2 + DAMP[3] * u3
                damp_v = (2 * DAMP[0]) * vv + DAMP[1] * v1 + DAMP[2] * v2 + DAMP[3] * v3
                laplace = (2 * LAP[0]) * uv + LAP[1] * u1 + LAP[2] * u2
                rt[f, t] = damp_u - 2.0 * lapse * vv
                rt[f + HALF, t] = damp_v + drag * vv - 0.5 * lapse * laplace

    load_base.wait()
    load_accum.wait()

    @pl.when(is_mid)
    def _():
        pltpu.make_async_copy(rb.at[pl.ds(0, 63)], rb.at[pl.ds(0, 63)], r_1).wait()
        kind = (u < 30) & (lax.rem(u, 6) < 3)

        @pl.loop(0, 64, unroll=8)
        def _(g):
            fb[g] = jnp.where(kind, rb[tab[0, 0, g]], rb[tab[1, 0, g]])

        @pl.loop(1, 64)
        def _(k):
            peer = lax.rem(me + k, 64)
            pltpu.make_async_remote_copy(
                fb.at[peer], gb.at[my_g], s_2, r_2, device_id={"gz": peer}, device_id_type=MESH).start()

        pltpu.make_async_copy(fb.at[me], gb.at[my_g], s_self).start()

    for s in send_x:
        s.wait_recv()
    for f in range(0, FIELDS, 2):
        hi, lo = xr[0, f // 2], xr[1, f // 2]
        xp[f, pl.ds(88, 8), :] = hi
        xp[f + 1, pl.ds(88, 8), :] = pltpu.roll(hi, 4, axis=0)
        xp[f, pl.ds(0, 8), :] = pltpu.roll(lo, 4, axis=0)
        xp[f + 1, pl.ds(0, 8), :] = lo

    @pl.loop(0, HALF)
    def _(f):
        for t in range(8):
            xg, q = t // 4, t % 4

            def shifted(field, k):
                return xp[field, pl.ds(16 + xg * 32 + 4 * k + q, 8, stride=4), :]

            def three(field):
                return [shifted(field, k) + shifted(field, -k) for k in (1, 2, 3)]

            uv, vv = shifted(f, 0), shifted(f + HALF, 0)
            u1, u2, u3 = three(f)
            v1, v2, v3 = three(f + HALF)
            damp_u = DAMP[0] * uv + DAMP[1] * u1 + DAMP[2] * u2 + DAMP[3] * u3
            damp_v = DAMP[0] * vv + DAMP[1] * v1 + DAMP[2] * v2 + DAMP[3] * v3
            laplace = LAP[0] * uv + LAP[1] * u1 + LAP[2] * u2
            rate_u = rt[f, t] + damp_u
            rate_v = rt[f + HALF, t] + damp_v - 0.5 * lap[t] * laplace
            rows = pl.ds(xg * 32 + q, 8, stride=4)
            for field, rate in ((f, rate_u), (f + HALF, rate_v)):
                bs[field, rows, :] = bs[field, rows, :] + C1 * rate
                ac[field, rows, :] = ac[field, rows, :] + C2 * rate

    out_1 = pltpu.make_async_copy(bs, q1, s_out.at[0])
    out_2 = pltpu.make_async_copy(ac, q2, s_out.at[1])
    out_3 = pltpu.make_async_copy(lap.at[pl.ds(0, 8)], lapse_out, s_out.at[2])
    out_1.start()
    out_2.start()
    out_3.start()
    send_y.wait_send()
    for s in send_x:
        s.wait_send()
    out_1.wait()
    out_2.wait()
    out_3.wait()

    @pl.when(is_mid)
    def _():
        pltpu.make_async_copy(mb.at[pl.ds(0, 39)], mb.at[pl.ds(0, 39)], s_1).wait()
        pltpu.make_async_copy(fb.at[pl.ds(0, 63)], fb.at[pl.ds(0, 63)], s_2).wait()
        pltpu.make_async_copy(fb.at[0], gb.at[0], s_self).wait()
        pltpu.make_async_copy(gb.at[pl.ds(0, 39)], gb.at[pl.ds(0, 39)], r_2).wait()

    @pl.when(jnp.logical_not(is_mid))
    def _():
        pltpu.make_async_copy(mb, mb, s_1).wait()
        pltpu.make_async_copy(gb, gb, r_2).wait()


def kernel_b(q1, q2, gb, lapse, o1, o2):
    b = lane_iota() % 32
    zero = jnp.zeros((8, LANES), jnp.float32)
    ups = [jnp.where(b >= 32 - k, 1.0, zero) for k in (1, 2, 3)]
    downs = [jnp.where(b < k, 1.0, zero) for k in (1, 2, 3)]
    for n in range(24):
        p, r = n // 5, n % 5
        t = n % 8
        xg, q = t // 4, t % 4
        rows = pl.ds(xg * 32 + q, 8, stride=4)

        def three(half):
            v = gb[half, 0, p]
            return [roll(v, -6 * r - k) * ups[k - 1] + roll(v, -6 * r + k) * downs[k - 1] for k in (1, 2, 3)]

        u1, u2, u3 = three(0)
        v1, v2, v3 = three(1)
        rate_u = DAMP[1] * u1 + DAMP[2] * u2 + DAMP[3] * u3
        rate_v = DAMP[1] * v1 + DAMP[2] * v2 + DAMP[3] * v3 - 0.5 * lapse[t] * (LAP[1] * u1 + LAP[2] * u2)
        for half, rate in ((0, rate_u), (1, rate_v)):
            o1[half, n // 8, rows, :] = q1[half, n // 8, rows, :] + C1 * rate
            o2[half, n // 8, rows, :] = q2[half, n // 8, rows, :] + C2 * rate


def local(state, base, accum, owner):
    shape = state.shape
    f32 = jnp.float32
    rows = (FIELDS, 64, LANES)
    any_spec = pl.BlockSpec(memory_space=pl.ANY)
    dma = pltpu.SemaphoreType.DMA
    q1, q2, gb, lapse = pl.pallas_call(
        kernel_a,
        out_shape=(
            jax.ShapeDtypeStruct(rows, f32),
            jax.ShapeDtypeStruct(rows, f32),
            jax.ShapeDtypeStruct((MIDS, 8, LANES), f32),
            jax.ShapeDtypeStruct((8, 8, LANES), f32),
        ),
        in_specs=[any_spec, any_spec, any_spec, pl.BlockSpec(memory_space=pltpu.SMEM)],
        out_specs=(any_spec,) * 4,
        scratch_shapes=[
            pltpu.VMEM((FIELDS, 96, LANES), f32),
            pltpu.VMEM(rows, f32),
            pltpu.VMEM(rows, f32),
            pltpu.VMEM(rows, f32),
            pltpu.VMEM((FIELDS, 8, 8, LANES), f32),
            pltpu.VMEM((16, 8, LANES), f32),
            pltpu.VMEM((MIDS, 8, LANES), f32),
            pltpu.VMEM((64, 8, LANES), f32),
            pltpu.VMEM((64, 8, LANES), f32),
            pltpu.VMEM((2, 12, 8, LANES), f32),
            pltpu.VMEM((2, 12, 8, LANES), f32),
            pltpu.VMEM((2, 8, LANES), jnp.int32),
            pltpu.SMEM((2, 8, LANES), jnp.int32),
            dma((3,)), dma, dma((3,)), dma, dma, dma((3,)), dma((3,)), dma, dma, dma, dma, dma,
        ],
        compiler_params=pltpu.CompilerParams(collective_id=0, has_side_effects=True, vmem_limit_bytes=24 << 20),
    )(state.reshape(rows), base.reshape(rows), accum.reshape(rows), owner)
    split = (2, HALF, 64, LANES)
    block = pl.BlockSpec((2, 3, 64, LANES), lambda i: (0, i, 0, 0))
    o1, o2 = pl.pallas_call(
        kernel_b,
        grid=(4,),
        out_shape=(jax.ShapeDtypeStruct(split, f32),) * 2,
        in_specs=[block, block,
                  pl.BlockSpec((2, 1, 5, 8, LANES), lambda i: (0, i, 0, 0, 0)),
                  pl.BlockSpec((8, 8, LANES), lambda i: (0, 0, 0))],
        out_specs=(block, block),
        compiler_params=pltpu.CompilerParams(dimension_semantics=("arbitrary",), vmem_limit_bytes=24 << 20),
    )(q1.reshape(split), q2.reshape(split), gb.reshape(2, 4, 5, 8, LANES), lapse)
    return o1.reshape(shape), o2.reshape(shape)


def solution(mesh):
    spec = P(None, "gx", ("gy", "gz"), None)
    return jax.shard_map(
        local, mesh=mesh, in_specs=(spec, spec, spec, P()), out_specs=(spec, spec), check_vma=False)
```

time: 160 us -> 36 us (0.23)
  local copies, waits for them, and re-layouts: 64.5 us -> 4.05 us
  other arithmetic: 60.1 us -> 0 us
  Pallas kernels: 0 us -> 31.1 us
  starting transfers between devices: 29.2 us -> 0 us
  waiting for transfers between devices: 4.42 us -> 0 us
    add x6 -> x0, other arithmetic: 36.5 us -> none  [the longest x1 21.6 us: local(): damping = damping + damping_part]
    pallas_call x0 -> x2, Pallas kernels: none -> 31.1 us  [the longest x1 28.3 us: local(): pl.pallas_call(kernel_a, out_shape=(jax.ShapeDtypeStruct(rows, f32), jax....]
    all_to_all x2 -> x0, starting transfers between devices: 24.7 us -> none  [the longest x1 13.6 us: local(): lax.all_to_all(outgoing, 'gz', split_axis=0, concat_axis=0, tiled=True)]
    slice x9 -> x0, local copies, waits for them, and re-layouts: 21.8 us -> none  [the longest x2 11 us: axis_terms(): lax.slice_in_dim(extended, 3 + offset, 3 + offset + length, axis=dimension)]
    another operation x5 -> x0, local copies, waits for them, and re-layouts: 18.6 us -> none  [the longest x2 8.07 us: local(): faces = jnp.stack([low_face, high_face])]
    mul x3 -> x0, other arithmetic: 16.7 us -> none  [the longest x1 12.6 us: axis_terms(): 30.0 * values[3]]
    mul x2 -> x0, local copies, waits for them, and re-layouts: 5.48 us -> none  [the longest x1 3.41 us: local(): next_section = base + SECTION_SHIFT * TIME_STEP * rate_values]
    ppermute x4 -> x0, starting transfers between devices: 4.49 us -> none  [the longest x2 3.41 us: extended_2(): lax.ppermute(lax.slice_in_dim(block, block.shape[dim] - width, None, axis...]
  transfers between devices with their start and end apart: 6 -> 0, of which waited for: 1 -> 0; matrix products, arithmetic and copies ran while one was open for 30% -> 0% of each run, Pallas kernels for 0% -> 0%
where the time goes in v1:
time: 36 us; the launch traced here: 35.8 us
  Pallas kernels  31.1 us (86%)
  local copies, waits for them, and re-layouts  4.05 us (11%)
  between operations  0.65 us (2%)
    pallas_call x1, Pallas kernels, local(): pl.pallas_call(kernel_a, out_shape=(jax.ShapeDtypeStruct(rows, f32), jax....  28.3 us
    unnamed x8, local copies, waits for them, and re-layouts  4.05 us
    pallas_call x1, Pallas kernels, local(): pl.pallas_call(kernel_b, grid=(4,), out_shape=(jax.ShapeDtypeStruct(split...  2.82 us

profile of v1, /device:TPU:1, one launch (start us, length us, event | category | flops | bytes accessed | tf_op | source)
XLA Modules:
  0.0 35.8 jit_solution(11278387319178989769)
XLA Ops:
  0.6 0.0 copy-start.3
  0.6 0.6 %copy-done.3 = s32[64]{0:T(128)S(1)} copy-done((s32[64]{0:T(128)S(1)}, s32[64]{0:T(128)}, u32[]{:S(2)}) %copy-start.3) | copy-done | bytes 280
  1.3 0.0 copy-start
  1.3 1.1 %copy-done = f32[24,16,1,512]{3,2,1,0:T(1,128)S(1)} copy-done((f32[24,16,1,512]{3,2,1,0:T(1,128)S(1)}, f32[24,16,1,512]{3,2,1,0:T(1,128)}, u32[]{:S(2)}) %copy-start) | copy-done | bytes 786456
  2.4 0.0 copy-start.1
  2.4 1.1 %copy-done.1 = f32[24,16,1,512]{3,2,1,0:T(1,128)S(1)} copy-done((f32[24,16,1,512]{3,2,1,0:T(1,128)S(1)}, f32[24,16,1,512]{3,2,1,0:T(1,128)}, u32[]{:S(2)}) %copy-start.1) | copy-done | bytes 786456
  3.6 0.0 copy-start.2
  3.6 1.1 %copy-done.2 = f32[24,16,1,512]{3,2,1,0:T(1,128)S(1)} copy-done((f32[24,16,1,512]{3,2,1,0:T(1,128)S(1)}, f32[24,16,1,512]{3,2,1,0:T(1,128)}, u32[]{:S(2)}) %copy-start.2) | copy-done | bytes 786456
  4.7 28.3 %shard_map.59 = (f32[24,64,128]{2,1,0:T(8,128)S(1)}, f32[24,64,128]{2,1,0:T(8,128)S(1)}, f32[40,8,128]{2,1,0:T(8,128)S(1)}, f32[8,8,128]{2,1,0:T(8,128)S(1)}) custom-call(f32[24,64,128]{2,1,0:T(8,128)S(1)} %bitcast.8, f32[24,64,128]{2,1,0:T(8,128)S(1)} %bitcast.9, f32[24,64,128]{2,1,0:T(8,128)S(1)} %bitcast.10, s32[64]{0:T(128)S(1)} %copy-done.3), custom_call_target="tpu_custom_call" | custom-call | tf_op jit(solution)/shard_map/pallas_call | solution.py:292
  33.0 2.8 %shard_map.60 = (f32[2,12,64,128]{3,2,1,0:T(8,128)}, f32[2,12,64,128]{3,2,1,0:T(8,128)}) custom-call(f32[2,12,64,128]{3,2,1,0:T(8,128)S(1)} %bitcast.11, f32[2,12,64,128]{3,2,1,0:T(8,128)S(1)} %bitcast.12, f32[2,4,5,8,128]{4,3,2,1,0:T(8,128)S(1)} %bitcast.13, f32[8,8,128]{2,1,0:T(8,128)S(1)} %get-tuple-element.11.lapse), custom_call_target="tpu_custom_call" | custom-call | tf_op jit(solution)/shard_map/pallas_call | solution.py:322
Async XLA Ops:
  0.6 0.7 %copy-start.3 = (s32[64]{0:T(128)S(1)}, s32[64]{0:T(128)}, u32[]{:S(2)}) copy-start(s32[64]{0:T(128)} %owner.1) | copy-start | bytes 772
  1.3 1.1 %copy-start = (f32[24,16,1,512]{3,2,1,0:T(1,128)S(1)}, f32[24,16,1,512]{3,2,1,0:T(1,128)}, u32[]{:S(2)}) copy-start(f32[24,16,1,512]{3,2,1,0:T(1,128)} %param.4) | copy-start | bytes 2359300
  2.4 1.1 %copy-start.1 = (f32[24,16,1,512]{3,2,1,0:T(1,128)S(1)}, f32[24,16,1,512]{3,2,1,0:T(1,128)}, u32[]{:S(2)}) copy-start(f32[24,16,1,512]{3,2,1,0:T(1,128)} %param.5) | copy-start | bytes 2359300
  3.6 1.1 %copy-start.2 = (f32[24,16,1,512]{3,2,1,0:T(1,128)S(1)}, f32[24,16,1,512]{3,2,1,0:T(1,128)}, u32[]{:S(2)}) copy-start(f32[24,16,1,512]{3,2,1,0:T(1,128)} %param.6) | copy-start | bytes 2359300

commit v2 on v1

v2 whole, which is shorter than its diff:
```python
import functools

import jax
import jax.numpy as jnp
from jax import lax
from jax.experimental import pallas as pl
from jax.experimental.pallas import tpu as pltpu
from jax.sharding import PartitionSpec as P

MESH = pl.DeviceIdType.MESH
FIELDS, HALF = 24, 12
LANES = 128
C1 = 0.5 * 0.25
C2 = 0.25 / 3.0
DAMP = (-20.0 / 64.0, 15.0 / 64.0, -6.0 / 64.0, 1.0 / 64.0)
LAP = (-30.0 / 12.0, 16.0 / 12.0, -1.0 / 12.0)
FAR_FIRST = (4, 3, 5, 2, 6, 1, 7, 0)


def lane_iota(rows=8):
    return lax.broadcasted_iota(jnp.int32, (rows, LANES), 1)


def roll(v, s):
    s %= LANES
    return v if s == 0 else pltpu.roll(v, s, axis=1)


def kernel_a(state, base, accum, owner_hbm, q1, q2,
             xp, sy, rt, lap, mb, rb, fb, gb, xs, xr, tabv, tab, owner,
             s_in, s_tab, s_y, r_y, s_x, r_x, s_1, r_1, s_2, r_2):
    gx, gy, me = lax.axis_index("gx"), lax.axis_index("gy"), lax.axis_index("gz")
    z, w = me // 8, lax.rem(me, 8)

    load_state = pltpu.make_async_copy(state, xp.at[:, pl.ds(16, 64)], s_in.at[0])
    load_base = pltpu.make_async_copy(base, q1, s_in.at[1])
    load_accum = pltpu.make_async_copy(accum, q2, s_in.at[2])
    load_owner = pltpu.make_async_copy(owner_hbm, owner, s_in.at[3])
    load_state.start()
    load_owner.start()

    barrier = pltpu.get_barrier_semaphore()

    @pl.loop(1, 64)
    def _(k):
        pl.semaphore_signal(barrier, inc=1, device_id={"gz": lax.rem(me + k, 64)}, device_id_type=MESH)

    pl.semaphore_signal(barrier, inc=1, device_id={"gy": 1 - gy}, device_id_type=MESH)
    pl.semaphore_signal(barrier, inc=1, device_id={"gx": 1 - gx}, device_id_type=MESH)
    load_base.start()
    load_accum.start()

    load_owner.wait()
    lanes = lane_iota()
    below = jnp.zeros((8, LANES), jnp.int32)
    above = jnp.zeros((8, LANES), jnp.int32)
    for c in range(64):
        hit = lanes == owner[c]
        below = jnp.where(hit, owner[(c + 63) % 64], below)
        above = jnp.where(hit, owner[(c + 1) % 64], above)
    tabv[0] = below
    tabv[1] = above
    load_tab = pltpu.make_async_copy(tabv, tab, s_tab)

    b = lanes % 32
    u = (lanes + 3) % 32
    load_state.wait()
    load_tab.start()

    def row(t):
        return (t // 4) * 32 + t % 4

    def tile(f, t):
        return xp[f, pl.ds(16 + row(t), 8, stride=4), :]

    @pl.loop(0, 8)
    def _(t):
        for p in range(5):
            acc = jnp.zeros((8, LANES), jnp.float32)
            for r in range(5 if p < 4 else 4):
                v = tile(p * 5 + r, t)
                x = jnp.where(b < 3, roll(v, 32), roll(v, 96))
                window = (u + 32 - 6 * r) % 32 < 6
                acc = jnp.where(window, roll(x, 6 * r), acc)
            mb[pl.ds(t * 64 + p, 8, stride=8), :] = acc

    first = lax.broadcasted_iota(jnp.int32, (8, LANES), 0) < 4
    for f in range(0, FIELDS, 2):
        lo0, lo1 = xp[f, pl.ds(24, 8), :], xp[f + 1, pl.ds(24, 8), :]
        hi0, hi1 = xp[f, pl.ds(64, 8), :], xp[f + 1, pl.ds(64, 8), :]
        xs[0, f // 2] = jnp.where(first, lo0, pltpu.roll(lo1, 4, axis=0))
        xs[1, f // 2] = jnp.where(first, pltpu.roll(hi0, 4, axis=0), hi1)

    pl.semaphore_wait(barrier, 65)

    def five(ref, j):
        if ref.shape[0] == 64:
            return ref.at[j, pl.ds(0, 5)]
        return ref.at[pl.ds(pl.multiple_of(8 * j, 8), 5)]

    def spread(source, target, send, recv):
        for d in FAR_FIRST:
            @pl.loop(0, 8)
            def _(k):
                peer = lax.rem(z + d, 8) * 8 + lax.rem(w + k, 8)

                @pl.when(peer != me)
                def _():
                    pltpu.make_async_remote_copy(
                        five(source, peer), five(target, me), send, recv,
                        device_id={"gz": peer}, device_id_type=MESH).start()

        pltpu.make_async_copy(five(source, me), five(target, me), recv).start()

    spread(mb, rb, s_1, r_1)

    send_y = pltpu.make_async_remote_copy(
        xp.at[:, pl.ds(16, 64)], sy, s_y, r_y, device_id={"gy": 1 - gy}, device_id_type=MESH)
    send_y.start()
    send_x = [
        pltpu.make_async_remote_copy(
            xp.at[:, pl.ds(16, 8)], xp.at[:, pl.ds(80, 8)], s_x.at[0], r_x.at[0],
            device_id={"gx": 1 - gx}, device_id_type=MESH),
        pltpu.make_async_remote_copy(
            xp.at[:, pl.ds(72, 8)], xp.at[:, pl.ds(8, 8)], s_x.at[1], r_x.at[1],
            device_id={"gx": 1 - gx}, device_id_type=MESH),
        pltpu.make_async_remote_copy(
            xs, xr, s_x.at[2], r_x.at[2], device_id={"gx": 1 - gx}, device_id_type=MESH),
    ]
    for s in send_x:
        s.start()

    load_tab.wait()
    for t in range(8):
        lap[t] = 1.0 + 0.25 * jnp.tanh(tile(0, t))
        total = tile(12, t)
        for f in range(13, 24):
            total = total + tile(f, t)
        lap[8 + t] = lap[t] * (total * (1.0 / 12.0))

    low = [b >= k for k in (1, 2, 3)]
    high = [b < 32 - k for k in (1, 2, 3)]
    left = [lanes >= 32 * k for k in (1, 2, 3)]
    right = [lanes < 128 - 32 * k for k in (1, 2, 3)]

    def plane(f, xg):
        values = [sy[f, pl.ds(xg * 32 + 3, 8, stride=4), :]]
        values += [tile(f, xg * 4 + q) for q in range(4)]
        values += [sy[f, pl.ds(xg * 32, 8, stride=4), :]]
        turned = [[v] + [roll(v, 32 * j) for j in (1, 2, 3)] for v in values]
        sums = []
        for q in range(4):
            v = values[q + 1]
            three = []
            for k in (1, 2, 3):
                plus = jnp.where(right[k - 1], turned[q + 1][4 - k], turned[q + 2][4 - k])
                minus = jnp.where(left[k - 1], turned[q + 1][k], turned[q][k])
                up = jnp.where(high[k - 1], roll(v, -k), 0.0)
                down = jnp.where(low[k - 1], roll(v, k), 0.0)
                three.append((plus + minus) + (up + down))
            sums.append((v, three))
        return sums

    send_y.wait_recv()

    @pl.loop(0, HALF)
    def _(f):
        for xg in range(2):
            us, vs = plane(f, xg), plane(f + HALF, xg)
            for q in range(4):
                t = xg * 4 + q
                lapse, drag = lap[t], lap[8 + t]
                uv, (u1, u2, u3) = us[q]
                vv, (v1, v2, v3) = vs[q]
                damp_u = (2 * DAMP[0]) * uv + DAMP[1] * u1 + DAMP[2] * u2 + DAMP[3] * u3
                damp_v = (2 * DAMP[0]) * vv + DAMP[1] * v1 + DAMP[2] * v2 + DAMP[3] * v3
                laplace = (2 * LAP[0]) * uv + LAP[1] * u1 + LAP[2] * u2
                rt[f, t] = damp_u - 2.0 * lapse * vv
                rt[f + HALF, t] = damp_v + drag * vv - 0.5 * lapse * laplace

    load_base.wait()
    load_accum.wait()
    pltpu.make_async_copy(rb.at[pl.ds(0, 40)], rb.at[pl.ds(0, 40)], r_1).wait()
    kind = (u < 30) & (lax.rem(u, 6) < 3)

    @pl.loop(0, 64, unroll=8)
    def _(g):
        fb[g] = jnp.where(kind, rb[tab[0, 0, g]], rb[tab[1, 0, g]])

    spread(fb, gb, s_2, r_2.at[z])

    for s in send_x:
        s.wait_recv()
    for f in range(0, FIELDS, 2):
        hi, lo = xr[0, f // 2], xr[1, f // 2]
        xp[f, pl.ds(88, 8), :] = hi
        xp[f + 1, pl.ds(88, 8), :] = pltpu.roll(hi, 4, axis=0)
        xp[f, pl.ds(0, 8), :] = pltpu.roll(lo, 4, axis=0)
        xp[f + 1, pl.ds(0, 8), :] = lo

    def add(f, t, rate):
        rows = pl.ds(row(t), 8, stride=4)
        q1[f, rows, :] = q1[f, rows, :] + C1 * rate
        q2[f, rows, :] = q2[f, rows, :] + C2 * rate

    @pl.loop(0, HALF)
    def _(f):
        for t in range(8):
            def shifted(field, k):
                return xp[field, pl.ds(16 + row(t) + 4 * k, 8, stride=4), :]

            def three(field):
                return [shifted(field, k) + shifted(field, -k) for k in (1, 2, 3)]

            uv, vv = shifted(f, 0), shifted(f + HALF, 0)
            u1, u2, u3 = three(f)
            v1, v2, v3 = three(f + HALF)
            damp_u = DAMP[0] * uv + DAMP[1] * u1 + DAMP[2] * u2 + DAMP[3] * u3
            damp_v = DAMP[0] * vv + DAMP[1] * v1 + DAMP[2] * v2 + DAMP[3] * v3
            laplace = LAP[0] * uv + LAP[1] * u1 + LAP[2] * u2
            add(f, t, rt[f, t] + damp_u)
            add(f + HALF, t, rt[f + HALF, t] + damp_v - 0.5 * lap[t] * laplace)

    send_y.wait_send()
    for s in send_x:
        s.wait_send()
    everything = pltpu.make_async_copy(mb.at[pl.ds(0, 315)], mb.at[pl.ds(0, 315)], s_1)
    everything.wait()

    zero = jnp.zeros((8, LANES), jnp.float32)
    ups = [jnp.where(b >= 32 - k, 1.0, zero) for k in (1, 2, 3)]
    downs = [jnp.where(b < k, 1.0, zero) for k in (1, 2, 3)]

    @pl.loop(0, 8)
    def _(k):
        near = lax.rem(k, 2) * ((k + 1) // 2) + (1 - lax.rem(k, 2)) * (8 - k // 2)
        t = lax.rem(z + near, 8)
        pltpu.make_async_copy(gb.at[pl.ds(0, 40)], gb.at[pl.ds(0, 40)], r_2.at[t]).wait()
        packed = [gb[pl.ds(t * 64 + p, 8, stride=8), :] for p in range(5)]
        lapse = lap[t]

        def three(f):
            v, r = packed[f // 5], f % 5
            return [roll(v, -6 * r - k) * ups[k - 1] + roll(v, -6 * r + k) * downs[k - 1] for k in (1, 2, 3)]

        for f in range(HALF):
            u1, u2, u3 = three(f)
            v1, v2, v3 = three(f + HALF)
            add(f, t, DAMP[1] * u1 + DAMP[2] * u2 + DAMP[3] * u3)
            add(f + HALF, t,
                DAMP[1] * v1 + DAMP[2] * v2 + DAMP[3] * v3 - 0.5 * lapse * (LAP[1] * u1 + LAP[2] * u2))

    pltpu.make_async_copy(mb.at[pl.ds(0, 315)], mb.at[pl.ds(0, 315)], s_2).wait()


PIECES = 4


def kernel_b(q1, q2, o1, o2, sems):
    copies = []
    for i in range(PIECES):
        part = pl.ds(i * (FIELDS // PIECES), FIELDS // PIECES)
        copies.append(pltpu.make_async_copy(q1.at[part], o1.at[part], sems.at[0, i]))
        copies.append(pltpu.make_async_copy(q2.at[part], o2.at[part], sems.at[1, i]))
    for c in copies:
        c.start()
    for c in copies:
        c.wait()


def local(state, base, accum, owner):
    shape = state.shape
    f32 = jnp.float32
    rows = (FIELDS, 64, LANES)
    hbm = pl.BlockSpec(memory_space=pltpu.HBM)
    vmem = pl.BlockSpec(memory_space=pltpu.VMEM)
    dma = pltpu.SemaphoreType.DMA
    in_hbm = [pltpu.with_memory_space_constraint(v, pltpu.HBM)
              for v in (state.reshape(rows), base.reshape(rows), accum.reshape(rows), owner)]
    q1, q2 = pl.pallas_call(
        kernel_a,
        out_shape=(pltpu.VMEM(rows, f32), pltpu.VMEM(rows, f32)),
        in_specs=[hbm] * 4,
        out_specs=(vmem, vmem),
        scratch_shapes=[
            pltpu.VMEM((FIELDS, 96, LANES), f32),
            pltpu.VMEM(rows, f32),
            pltpu.VMEM((FIELDS, 8, 8, LANES), f32),
            pltpu.VMEM((16, 8, LANES), f32),
            pltpu.VMEM((512, LANES), f32),
            pltpu.VMEM((64, 8, LANES), f32),
            pltpu.VMEM((64, 8, LANES), f32),
            pltpu.VMEM((512, LANES), f32),
            pltpu.VMEM((2, 12, 8, LANES), f32),
            pltpu.VMEM((2, 12, 8, LANES), f32),
            pltpu.VMEM((2, 8, LANES), jnp.int32),
            pltpu.SMEM((2, 8, LANES), jnp.int32),
            pltpu.SMEM((64,), jnp.int32),
            dma((4,)), dma, dma, dma, dma((3,)), dma((3,)), dma, dma, dma, dma((8,)),
        ],
        compiler_params=pltpu.CompilerParams(collective_id=0, has_side_effects=True, vmem_limit_bytes=24 << 20),
    )(*in_hbm)
    o1, o2 = pl.pallas_call(
        kernel_b,
        out_shape=(jax.ShapeDtypeStruct(rows, f32),) * 2,
        in_specs=[vmem, vmem],
        out_specs=(hbm, hbm),
        scratch_shapes=[dma((2, PIECES))],
        compiler_params=pltpu.CompilerParams(vmem_limit_bytes=24 << 20),
    )(q1, q2)
    return o1.reshape(shape), o2.reshape(shape)


def solution(mesh):
    spec = P(None, "gx", ("gy", "gz"), None)
    return jax.shard_map(
        local, mesh=mesh, in_specs=(spec, spec, spec, P()), out_specs=(spec, spec), check_vma=False)
```

time: 36 us -> 28.4 us (0.79)
  local copies, waits for them, and re-layouts: 4.05 us -> 0 us
  Pallas kernels: 31.1 us -> 27.6 us
    unnamed x8 -> x0, local copies, waits for them, and re-layouts: 4.05 us -> none
    pallas_call x2, Pallas kernels: 31.1 us -> 27.6 us  [the longest x1 26.4 us: local(): pl.pallas_call(kernel_a, out_shape=(pltpu.VMEM(rows, f32), pltpu.VMEM(row...]
where the time goes in v2:
time: 28.4 us; the launch traced here: 28.3 us
  Pallas kernels  27.6 us (97%)
  between operations  0.64 us (2%)
    pallas_call x1, Pallas kernels, local(): pl.pallas_call(kernel_a, out_shape=(pltpu.VMEM(rows, f32), pltpu.VMEM(row...  26.4 us
    pallas_call x1, Pallas kernels, local(): pl.pallas_call(kernel_b, out_shape=(jax.ShapeDtypeStruct(rows, f32),) * 2...  1.2 us

profile of v2, /device:TPU:1, one launch (start us, length us, event | category | flops | bytes accessed | tf_op | source)
XLA Modules:
  0.0 28.3 jit_solution(2321547699693869279)
XLA Ops:
  0.6 26.4 %shard_map.59 = (f32[24,64,128]{2,1,0:T(8,128)S(1)}, f32[24,64,128]{2,1,0:T(8,128)S(1)}) custom-call(f32[24,64,128]{2,1,0:T(8,128)} %bitcast.5, f32[24,64,128]{2,1,0:T(8,128)} %bitcast.6, f32[24,64,128]{2,1,0:T(8,128)} %bitcast.7, s32[64]{0:T(128)} %owner_hbm.1), custom_call_target="tpu_custom_call" | custom-call | tf_op jit(solution)/shard_map/pallas_call | solution.py:280
  27.1 1.2 %shard_map.60 = (f32[24,64,128]{2,1,0:T(8,128)}, f32[24,64,128]{2,1,0:T(8,128)}) custom-call(f32[24,64,128]{2,1,0:T(8,128)S(1)} %get-tuple-element.6.q1, f32[24,64,128]{2,1,0:T(8,128)S(1)} %get-tuple-element.7.q2), custom_call_target="tpu_custom_call" | custom-call | tf_op jit(solution)/shard_map/pallas_call | solution.py:303

commit v3 on v2

--- a/solution.py
+++ b/solution.py
@@ -14,6 +14,8 @@
 C2 = 0.25 / 3.0
 DAMP = (-20.0 / 64.0, 15.0 / 64.0, -6.0 / 64.0, 1.0 / 64.0)
 LAP = (-30.0 / 12.0, 16.0 / 12.0, -1.0 / 12.0)
+ALPHA = LAP[2] / DAMP[3]
+BETA = (LAP[1] - LAP[2] * DAMP[2] / DAMP[3]) / DAMP[3]
 FAR_FIRST = (4, 3, 5, 2, 6, 1, 7, 0)
 
 
@@ -41,9 +43,15 @@
 
     barrier = pltpu.get_barrier_semaphore()
 
-    @pl.loop(1, 64)
-    def _(k):
-        pl.semaphore_signal(barrier, inc=1, device_id={"gz": lax.rem(me + k, 64)}, device_id_type=MESH)
+    def each_peer(action):
+        for d in FAR_FIRST:
+            @pl.loop(0 if d else 1, 8)
+            def _(k):
+                action(lax.rem(z + d, 8) * 8 + lax.rem(w + k, 8))
+
+    @each_peer
+    def _(peer):
+        pl.semaphore_signal(barrier, inc=1, device_id={"gz": peer}, device_id_type=MESH)
 
     pl.semaphore_signal(barrier, inc=1, device_id={"gy": 1 - gy}, device_id_type=MESH)
     pl.semaphore_signal(barrier, inc=1, device_id={"gx": 1 - gx}, device_id_type=MESH)
@@ -73,13 +81,19 @@
     def tile(f, t):
         return xp[f, pl.ds(16 + row(t), 8, stride=4), :]
 
+    zero = jnp.zeros((8, LANES), jnp.float32)
+    to_high = [jnp.where(b >= 32 - k, DAMP[k], zero) for k in (1, 2, 3)]
+    to_low = [jnp.where(b < k, DAMP[k], zero) for k in (1, 2, 3)]
+
     @pl.loop(0, 8)
     def _(t):
         for p in range(5):
-            acc = jnp.zeros((8, LANES), jnp.float32)
+            acc = zero
             for r in range(5 if p < 4 else 4):
                 v = tile(p * 5 + r, t)
-                x = jnp.where(b < 3, roll(v, 32), roll(v, 96))
+                x = zero
+                for k in (1, 2, 3):
+                    x = x + to_high[k - 1] * roll(v, 32 - k) + to_low[k - 1] * roll(v, k - 32)
                 window = (u + 32 - 6 * r) % 32 < 6
                 acc = jnp.where(window, roll(x, 6 * r), acc)
             mb[pl.ds(t * 64 + p, 8, stride=8), :] = acc
@@ -99,16 +113,11 @@
         return ref.at[pl.ds(pl.multiple_of(8 * j, 8), 5)]
 
     def spread(source, target, send, recv):
-        for d in FAR_FIRST:
-            @pl.loop(0, 8)
-            def _(k):
-                peer = lax.rem(z + d, 8) * 8 + lax.rem(w + k, 8)
-
-                @pl.when(peer != me)
-                def _():
-                    pltpu.make_async_remote_copy(
-                        five(source, peer), five(target, me), send, recv,
-                        device_id={"gz": peer}, device_id_type=MESH).start()
+        @each_peer
+        def _(peer):
+            pltpu.make_async_remote_copy(
+                five(source, peer), five(target, me), send, recv,
+                device_id={"gz": peer}, device_id_type=MESH).start()
 
         pltpu.make_async_copy(five(source, me), five(target, me), recv).start()
 
@@ -185,7 +194,7 @@
 
     @pl.loop(0, 64, unroll=8)
     def _(g):
-        fb[g] = jnp.where(kind, rb[tab[0, 0, g]], rb[tab[1, 0, g]])
+        fb[g] = jnp.where(kind, rb[tab[1, 0, g]], rb[tab[0, 0, g]])
 
     spread(fb, gb, s_2, r_2.at[z])
 
@@ -227,9 +236,13 @@
     everything = pltpu.make_async_copy(mb.at[pl.ds(0, 315)], mb.at[pl.ds(0, 315)], s_1)
     everything.wait()
 
-    zero = jnp.zeros((8, LANES), jnp.float32)
-    ups = [jnp.where(b >= 32 - k, 1.0, zero) for k in (1, 2, 3)]
-    downs = [jnp.where(b < k, 1.0, zero) for k in (1, 2, 3)]
+    slot = lax.rem(u, 6)
+    edge = (b < 3) | (b >= 29)
+    edge_1, edge_2 = jnp.where(edge, C1, zero), jnp.where(edge, C2, zero)
+    next_up = jnp.where((slot == 3) | (slot == 4), ALPHA, zero)
+    next_down = jnp.where((slot == 1) | (slot == 2), ALPHA, zero)
+    second_up = jnp.where(slot == 3, BETA, zero)
+    second_down = jnp.where(slot == 2, BETA, zero)
 
     @pl.loop(0, 8)
     def _(k):
@@ -237,18 +250,21 @@
         t = lax.rem(z + near, 8)
         pltpu.make_async_copy(gb.at[pl.ds(0, 40)], gb.at[pl.ds(0, 40)], r_2.at[t]).wait()
         packed = [gb[pl.ds(t * 64 + p, 8, stride=8), :] for p in range(5)]
-        lapse = lap[t]
-
-        def three(f):
-            v, r = packed[f // 5], f % 5
-            return [roll(v, -6 * r - k) * ups[k - 1] + roll(v, -6 * r + k) * downs[k - 1] for k in (1, 2, 3)]
+        half_lapse = -0.5 * lap[t]
+        laplaces = [
+            roll(v, -1) * next_up + roll(v, 1) * next_down + roll(v, -2) * second_up + roll(v, 2) * second_down
+            for v in packed[:3]
+        ]
+        rows = pl.ds(row(t), 8, stride=4)
+
+        def add_edge(f, rate):
+            q1[f, rows, :] = q1[f, rows, :] + edge_1 * rate
+            q2[f, rows, :] = q2[f, rows, :] + edge_2 * rate
 
         for f in range(HALF):
-            u1, u2, u3 = three(f)
-            v1, v2, v3 = three(f + HALF)
-            add(f, t, DAMP[1] * u1 + DAMP[2] * u2 + DAMP[3] * u3)
-            add(f + HALF, t,
-                DAMP[1] * v1 + DAMP[2] * v2 + DAMP[3] * v3 - 0.5 * lapse * (LAP[1] * u1 + LAP[2] * u2))
+            g = f + HALF
+            add_edge(f, roll(packed[f // 5], -6 * (f % 5)))
+            add_edge(g, roll(packed[g // 5], -6 * (g % 5)) + half_lapse * roll(laplaces[f // 5], -6 * (f % 5)))
 
     pltpu.make_async_copy(mb.at[pl.ds(0, 315)], mb.at[pl.ds(0, 315)], s_2).wait()
 

time: 28.4 us -> 27.8 us (0.979); the launches traced: 28.3 us -> 27.3 us
  Pallas kernels: 27.6 us -> 26.6 us
    pallas_call x1, Pallas kernels: 26.4 us -> 25.4 us  [local(): pl.pallas_call(kernel_a, out_shape=(pltpu.VMEM(rows, f32), pltpu.VMEM(row...]
where the time goes in v3:
time: 27.8 us; the launch traced here: 27.3 us
  Pallas kernels  26.6 us (96%)
  between operations  0.64 us (2%)
    pallas_call x1, Pallas kernels, local(): pl.pallas_call(kernel_a, out_shape=(pltpu.VMEM(rows, f32), pltpu.VMEM(row...  25.4 us
    pallas_call x1, Pallas kernels, local(): pl.pallas_call(kernel_b, out_shape=(jax.ShapeDtypeStruct(rows, f32),) * 2...  1.2 us

profile of v3, /device:TPU:1, one launch (start us, length us, event | category | flops | bytes accessed | tf_op | source)
XLA Modules:
  0.0 27.3 jit_solution(12231735594553152156)
XLA Ops:
  0.6 25.4 %shard_map.59 = (f32[24,64,128]{2,1,0:T(8,128)S(1)}, f32[24,64,128]{2,1,0:T(8,128)S(1)}) custom-call(f32[24,64,128]{2,1,0:T(8,128)} %bitcast.5, f32[24,64,128]{2,1,0:T(8,128)} %bitcast.6, f32[24,64,128]{2,1,0:T(8,128)} %bitcast.7, s32[64]{0:T(128)} %owner_hbm.1), custom_call_target="tpu_custom_call" | custom-call | tf_op jit(solution)/shard_map/pallas_call | solution.py:296
  26.1 1.2 %shard_map.60 = (f32[24,64,128]{2,1,0:T(8,128)}, f32[24,64,128]{2,1,0:T(8,128)}) custom-call(f32[24,64,128]{2,1,0:T(8,128)S(1)} %get-tuple-element.6.q1, f32[24,64,128]{2,1,0:T(8,128)S(1)} %get-tuple-element.7.q2), custom_call_target="tpu_custom_call" | custom-call | tf_op jit(solution)/shard_map/pallas_call | solution.py:319

commit v4 on v3

--- a/solution.py
+++ b/solution.py
@@ -16,7 +16,17 @@
 LAP = (-30.0 / 12.0, 16.0 / 12.0, -1.0 / 12.0)
 ALPHA = LAP[2] / DAMP[3]
 BETA = (LAP[1] - LAP[2] * DAMP[2] / DAMP[3]) / DAMP[3]
-FAR_FIRST = (4, 3, 5, 2, 6, 1, 7, 0)
+P2_ORDER = (0, 1, 2, 3, 4, 7, 5, 6)
+REACH = 3
+
+
+def hops(dz, dy, dx):
+    return min(dz, 8 - dz) + min(dy, 4 - dy) + dx
+
+
+NEAR = sorted(
+    ((dz, dy, dx) for dz in range(8) for dy in range(4) for dx in range(2) if hops(dz, dy, dx) <= REACH),
+    key=lambda d: -hops(*d))
 
 
 def lane_iota(rows=8):
@@ -30,9 +40,10 @@
 
 def kernel_a(state, base, accum, owner_hbm, q1, q2,
              xp, sy, rt, lap, mb, rb, fb, gb, xs, xr, tabv, tab, owner,
-             s_in, s_tab, s_y, r_y, s_x, r_x, s_1, r_1, s_2, r_2):
+             s_in, s_tab, s_y, r_y, s_x, r_x, s_1, r_1, s_2, r_2, beside, beyond):
     gx, gy, me = lax.axis_index("gx"), lax.axis_index("gy"), lax.axis_index("gz")
     z, w = me // 8, lax.rem(me, 8)
+    y, x = w // 2, lax.rem(w, 2)
 
     load_state = pltpu.make_async_copy(state, xp.at[:, pl.ds(16, 64)], s_in.at[0])
     load_base = pltpu.make_async_copy(base, q1, s_in.at[1])
@@ -43,16 +54,16 @@
 
     barrier = pltpu.get_barrier_semaphore()
 
-    def each_peer(action):
-        for d in FAR_FIRST:
-            @pl.loop(0 if d else 1, 8)
-            def _(k):
-                action(lax.rem(z + d, 8) * 8 + lax.rem(w + k, 8))
-
-    @each_peer
-    def _(peer):
-        pl.semaphore_signal(barrier, inc=1, device_id={"gz": peer}, device_id_type=MESH)
-
+    def device(dz, dy, dx):
+        return (z + dz) % 8 * 8 + (y + dy) % 4 * 2 + (x + dx) % 2
+
+    def pair_of(peer):
+        pz, py, px = peer // 8, peer % 8 // 2, peer % 2
+        half = pz // 4
+        return pz % 4 * 8 + (py + 2 * half) % 4 * 2 + (px + half) % 2
+
+    for d in NEAR[:-1]:
+        pl.semaphore_signal(barrier, inc=1, device_id={"gz": device(*d)}, device_id_type=MESH)
     pl.semaphore_signal(barrier, inc=1, device_id={"gy": 1 - gy}, device_id_type=MESH)
     pl.semaphore_signal(barrier, inc=1, device_id={"gx": 1 - gx}, device_id_type=MESH)
     load_base.start()
@@ -82,21 +93,32 @@
         return xp[f, pl.ds(16 + row(t), 8, stride=4), :]
 
     zero = jnp.zeros((8, LANES), jnp.float32)
-    to_high = [jnp.where(b >= 32 - k, DAMP[k], zero) for k in (1, 2, 3)]
-    to_low = [jnp.where(b < k, DAMP[k], zero) for k in (1, 2, 3)]
+    slot = lax.rem(u, 6)
+    to_high = [jnp.where((slot < 3) & (slot >= 3 - k), DAMP[k], zero) for k in (1, 2, 3)]
+    to_low = [jnp.where((slot >= 3) & (slot < 3 + k), DAMP[k], zero) for k in (1, 2, 3)]
+    windows = [(u + 32 - 6 * r) % 32 < 6 for r in range(5)]
 
     @pl.loop(0, 8)
     def _(t):
         for p in range(5):
-            acc = zero
+            faces = zero
             for r in range(5 if p < 4 else 4):
-                v = tile(p * 5 + r, t)
-                x = zero
-                for k in (1, 2, 3):
-                    x = x + to_high[k - 1] * roll(v, 32 - k) + to_low[k - 1] * roll(v, k - 32)
-                window = (u + 32 - 6 * r) % 32 < 6
-                acc = jnp.where(window, roll(x, 6 * r), acc)
-            mb[pl.ds(t * 64 + p, 8, stride=8), :] = acc
+                faces = jnp.where(windows[r], roll(tile(p * 5 + r, t), 6 * r), faces)
+            terms = [roll(faces, 32 - k) * to_high[k - 1] + roll(faces, k - 32) * to_low[k - 1] for k in (1, 2, 3)]
+            mb[pl.ds(t % 4 * 128 + t // 4 * 5 + p, 8, stride=16), :] = terms[0] + terms[1] + terms[2]
+
+    pl.semaphore_wait(barrier, 33)
+
+    def pair_rows(ref, j):
+        return ref.at[pl.ds(pl.multiple_of(16 * j, 8), 10)]
+
+    for d in NEAR[:-1]:
+        peer = device(*d)
+        pltpu.make_async_remote_copy(
+            pair_rows(mb, pair_of(peer)), rb.at[me, pl.ds(0, 10)], s_1, r_1,
+            device_id={"gz": peer}, device_id_type=MESH).start()
+    pltpu.make_async_copy(pair_rows(mb, pair_of(me)), rb.at[me, pl.ds(0, 10)], r_1).start()
+    pl.semaphore_signal(beside, inc=1, device_id={"gz": device(0, 0, 1)}, device_id_type=MESH)
 
     first = lax.broadcasted_iota(jnp.int32, (8, LANES), 0) < 4
     for f in range(0, FIELDS, 2):
@@ -104,24 +126,6 @@
         hi0, hi1 = xp[f, pl.ds(64, 8), :], xp[f + 1, pl.ds(64, 8), :]
         xs[0, f // 2] = jnp.where(first, lo0, pltpu.roll(lo1, 4, axis=0))
         xs[1, f // 2] = jnp.where(first, pltpu.roll(hi0, 4, axis=0), hi1)
-
-    pl.semaphore_wait(barrier, 65)
-
-    def five(ref, j):
-        if ref.shape[0] == 64:
-            return ref.at[j, pl.ds(0, 5)]
-        return ref.at[pl.ds(pl.multiple_of(8 * j, 8), 5)]
-
-    def spread(source, target, send, recv):
-        @each_peer
-        def _(peer):
-            pltpu.make_async_remote_copy(
-                five(source, peer), five(target, me), send, recv,
-                device_id={"gz": peer}, device_id_type=MESH).start()
-
-        pltpu.make_async_copy(five(source, me), five(target, me), recv).start()
-
-    spread(mb, rb, s_1, r_1)
 
     send_y = pltpu.make_async_remote_copy(
         xp.at[:, pl.ds(16, 64)], sy, s_y, r_y, device_id={"gy": 1 - gy}, device_id_type=MESH)
@@ -138,6 +142,9 @@
     ]
     for s in send_x:
         s.start()
+
+    pl.semaphore_wait(beside, 1)
+    pl.semaphore_signal(beyond, inc=1, device_id={"gz": device(6, 3, 0)}, device_id_type=MESH)
 
     load_tab.wait()
     for t in range(8):
@@ -189,14 +196,34 @@
 
     load_base.wait()
     load_accum.wait()
-    pltpu.make_async_copy(rb.at[pl.ds(0, 40)], rb.at[pl.ds(0, 40)], r_1).wait()
-    kind = (u < 30) & (lax.rem(u, 6) < 3)
-
-    @pl.loop(0, 64, unroll=8)
-    def _(g):
-        fb[g] = jnp.where(kind, rb[tab[1, 0, g]], rb[tab[0, 0, g]])
-
-    spread(fb, gb, s_2, r_2.at[z])
+    pltpu.make_async_copy(rb.at[pl.ds(0, 20)], rb.at[pl.ds(0, 20)], r_1).wait()
+    pl.semaphore_wait(beyond, 1)
+    kind = slot < 3
+    my_slot = z // 4 * 32 + pair_of(me)
+
+    def permute(plane):
+        for k in range(8):
+            g = plane * 8 + k
+            below_g, above_g = rb[tab[0, 0, g]], rb[tab[1, 0, g]]
+            fb[g] = jnp.concatenate(
+                [jnp.where(kind, above_g[h:h + 8], below_g[h:h + 8]) for h in (0, 8)], axis=0)
+
+    permute(P2_ORDER[0])
+    for n, plane in enumerate(P2_ORDER):
+        if n < 7:
+            permute(P2_ORDER[n + 1])
+
+        @pl.loop(0, 8)
+        def _(k):
+            peer = plane * 8 + k
+
+            @pl.when(peer != me)
+            def _():
+                pltpu.make_async_remote_copy(
+                    fb.at[peer, pl.ds(0, 10)], pair_rows(gb, my_slot), s_2, r_2.at[z],
+                    device_id={"gz": peer}, device_id_type=MESH).start()
+
+    pltpu.make_async_copy(fb.at[me, pl.ds(0, 10)], pair_rows(gb, my_slot), r_2.at[z]).start()
 
     for s in send_x:
         s.wait_recv()
@@ -233,10 +260,8 @@
     send_y.wait_send()
     for s in send_x:
         s.wait_send()
-    everything = pltpu.make_async_copy(mb.at[pl.ds(0, 315)], mb.at[pl.ds(0, 315)], s_1)
-    everything.wait()
-
-    slot = lax.rem(u, 6)
+    pltpu.make_async_copy(mb.at[pl.ds(0, 310)], mb.at[pl.ds(0, 310)], s_1).wait()
+
     edge = (b < 3) | (b >= 29)
     edge_1, edge_2 = jnp.where(edge, C1, zero), jnp.where(edge, C2, zero)
     next_up = jnp.where((slot == 3) | (slot == 4), ALPHA, zero)
@@ -244,12 +269,29 @@
     second_up = jnp.where(slot == 3, BETA, zero)
     second_down = jnp.where(slot == 2, BETA, zero)
 
-    @pl.loop(0, 8)
-    def _(k):
-        near = lax.rem(k, 2) * ((k + 1) // 2) + (1 - lax.rem(k, 2)) * (8 - k // 2)
-        t = lax.rem(z + near, 8)
-        pltpu.make_async_copy(gb.at[pl.ds(0, 40)], gb.at[pl.ds(0, 40)], r_2.at[t]).wait()
-        packed = [gb[pl.ds(t * 64 + p, 8, stride=8), :] for p in range(5)]
+    sub = lax.broadcasted_iota(jnp.int32, (8, LANES), 0)
+
+    def reached(neighbour, t):
+        nz, ny, nx = neighbour // 8, neighbour % 8 // 2, neighbour % 2
+        dz, dy = jnp.abs(nz - t), jnp.abs(sub // 2 - ny)
+        dx = jnp.abs(sub % 2 - nx)
+        return jnp.minimum(dz, 8 - dz) + jnp.minimum(dy, 4 - dy) + dx
+
+    chosen = []
+    for t in range(4):
+        chosen.append(jnp.where(kind, reached(tab[1, 0, me], t), reached(tab[0, 0, me], t)) <= REACH)
+
+    for t in (1, 5, 0, 4, 2, 6, 3, 7):
+        if t < 4:
+            for plane in (t, t + 4):
+                pltpu.make_async_copy(gb.at[pl.ds(0, 80)], gb.at[pl.ds(0, 80)], r_2.at[plane]).wait()
+        packed = []
+        for p in range(5):
+            start = t % 4 * 128 + t // 4 * 5 + p
+            packed.append(jnp.where(
+                chosen[t % 4],
+                gb[pl.ds(start, 8, stride=16), :],
+                gb[pl.ds(512 + start, 8, stride=16), :]))
         half_lapse = -0.5 * lap[t]
         laplaces = [
             roll(v, -1) * next_up + roll(v, 1) * next_down + roll(v, -2) * second_up + roll(v, 2) * second_down
@@ -266,10 +308,10 @@
             add_edge(f, roll(packed[f // 5], -6 * (f % 5)))
             add_edge(g, roll(packed[g // 5], -6 * (g % 5)) + half_lapse * roll(laplaces[f // 5], -6 * (f % 5)))
 
-    pltpu.make_async_copy(mb.at[pl.ds(0, 315)], mb.at[pl.ds(0, 315)], s_2).wait()
-
-
-PIECES = 4
+    pltpu.make_async_copy(gb.at[pl.ds(0, 630)], gb.at[pl.ds(0, 630)], s_2).wait()
+
+
+PIECES = 1
 
 
 def kernel_b(q1, q2, o1, o2, sems):
@@ -304,15 +346,16 @@
             pltpu.VMEM((FIELDS, 8, 8, LANES), f32),
             pltpu.VMEM((16, 8, LANES), f32),
             pltpu.VMEM((512, LANES), f32),
-            pltpu.VMEM((64, 8, LANES), f32),
-            pltpu.VMEM((64, 8, LANES), f32),
-            pltpu.VMEM((512, LANES), f32),
+            pltpu.VMEM((64, 16, LANES), f32),
+            pltpu.VMEM((64, 16, LANES), f32),
+            pltpu.VMEM((1024, LANES), f32),
             pltpu.VMEM((2, 12, 8, LANES), f32),
             pltpu.VMEM((2, 12, 8, LANES), f32),
             pltpu.VMEM((2, 8, LANES), jnp.int32),
             pltpu.SMEM((2, 8, LANES), jnp.int32),
             pltpu.SMEM((64,), jnp.int32),
             dma((4,)), dma, dma, dma, dma((3,)), dma((3,)), dma, dma, dma, dma((8,)),
+            pltpu.SemaphoreType.REGULAR, pltpu.SemaphoreType.REGULAR,
         ],
         compiler_params=pltpu.CompilerParams(collective_id=0, has_side_effects=True, vmem_limit_bytes=24 << 20),
     )(*in_hbm)

time: 27.8 us -> 27 us (0.971); the launches traced: 27.3 us -> 26.9 us
  Pallas kernels: 26.6 us -> 26.3 us
    pallas_call x1, Pallas kernels: 25.4 us -> 25.1 us  [local(): pl.pallas_call(kernel_a, out_shape=(pltpu.VMEM(rows, f32), pltpu.VMEM(row...]
where the time goes in v4:
time: 27 us; the launch traced here: 26.9 us
  Pallas kernels  26.3 us (97%)
  between operations  0.64 us (2%)
    pallas_call x1, Pallas kernels, local(): pl.pallas_call(kernel_a, out_shape=(pltpu.VMEM(rows, f32), pltpu.VMEM(row...  25.1 us
    pallas_call x1, Pallas kernels, local(): pl.pallas_call(kernel_b, out_shape=(jax.ShapeDtypeStruct(rows, f32),) * 2...  1.16 us

profile of v4, /device:TPU:1, one launch (start us, length us, event | category | flops | bytes accessed | tf_op | source)
XLA Modules:
  0.0 26.9 jit_solution(17115263477764410238)
XLA Ops:
  0.6 25.1 %shard_map.59 = (f32[24,64,128]{2,1,0:T(8,128)S(1)}, f32[24,64,128]{2,1,0:T(8,128)S(1)}) custom-call(f32[24,64,128]{2,1,0:T(8,128)} %bitcast.5, f32[24,64,128]{2,1,0:T(8,128)} %bitcast.6, f32[24,64,128]{2,1,0:T(8,128)} %bitcast.7, s32[64]{0:T(128)} %owner_hbm.1), custom_call_target="tpu_custom_call" | custom-call | tf_op jit(solution)/shard_map/pallas_call | solution.py:338
  25.8 1.2 %shard_map.60 = (f32[24,64,128]{2,1,0:T(8,128)}, f32[24,64,128]{2,1,0:T(8,128)}) custom-call(f32[24,64,128]{2,1,0:T(8,128)S(1)} %get-tuple-element.6.q1, f32[24,64,128]{2,1,0:T(8,128)S(1)} %get-tuple-element.7.q2), custom_call_target="tpu_custom_call" | custom-call | tf_op jit(solution)/shard_map/pallas_call | solution.py:362

commit v5 on v4

--- a/solution.py
+++ b/solution.py
@@ -54,13 +54,18 @@
 
     barrier = pltpu.get_barrier_semaphore()
 
+    zs = [lax.rem(z + d, 8) for d in range(8)]
+    ws = [[lax.rem(y + dy, 4) * 2 + lax.rem(x + dx, 2) for dx in range(2)] for dy in range(4)]
+    halves = [v // 4 for v in zs[:4]]
+    halves += [1 - v for v in halves]
+    planes = [lax.rem(z + d, 4) * 8 for d in range(4)]
+
     def device(dz, dy, dx):
-        return (z + dz) % 8 * 8 + (y + dy) % 4 * 2 + (x + dx) % 2
-
-    def pair_of(peer):
-        pz, py, px = peer // 8, peer % 8 // 2, peer % 2
-        half = pz // 4
-        return pz % 4 * 8 + (py + 2 * half) % 4 * 2 + (px + half) % 2
+        return zs[dz] * 8 + ws[dy][dx]
+
+    def pair_at(dz, dy, dx):
+        across = ws[(dy + 2) % 4][1 - dx] - ws[dy][dx]
+        return planes[dz % 4] + ws[dy][dx] + halves[dz] * across
 
     for d in NEAR[:-1]:
         pl.semaphore_signal(barrier, inc=1, device_id={"gz": device(*d)}, device_id_type=MESH)
@@ -115,9 +120,10 @@
     for d in NEAR[:-1]:
         peer = device(*d)
         pltpu.make_async_remote_copy(
-            pair_rows(mb, pair_of(peer)), rb.at[me, pl.ds(0, 10)], s_1, r_1,
+            pair_rows(mb, pair_at(*d)), rb.at[me, pl.ds(0, 10)], s_1, r_1,
             device_id={"gz": peer}, device_id_type=MESH).start()
-    pltpu.make_async_copy(pair_rows(mb, pair_of(me)), rb.at[me, pl.ds(0, 10)], r_1).start()
+    my_pair = pair_at(0, 0, 0)
+    pltpu.make_async_copy(pair_rows(mb, my_pair), rb.at[me, pl.ds(0, 10)], r_1).start()
     pl.semaphore_signal(beside, inc=1, device_id={"gz": device(0, 0, 1)}, device_id_type=MESH)
 
     first = lax.broadcasted_iota(jnp.int32, (8, LANES), 0) < 4
@@ -199,7 +205,7 @@
     pltpu.make_async_copy(rb.at[pl.ds(0, 20)], rb.at[pl.ds(0, 20)], r_1).wait()
     pl.semaphore_wait(beyond, 1)
     kind = slot < 3
-    my_slot = z // 4 * 32 + pair_of(me)
+    my_slot = z // 4 * 32 + my_pair
 
     def permute(plane):
         for k in range(8):

time: 27 us -> 26.7 us (0.989)
  Pallas kernels: 26.3 us -> 26 us
    pallas_call x1, Pallas kernels: 25.1 us -> 24.8 us  [local(): pl.pallas_call(kernel_a, out_shape=(pltpu.VMEM(rows, f32), pltpu.VMEM(row...]
where the time goes in v5:
time: 26.7 us; the launch traced here: 26.6 us
  Pallas kernels  26 us (97%)
  between operations  0.64 us (2%)
    pallas_call x1, Pallas kernels, local(): pl.pallas_call(kernel_a, out_shape=(pltpu.VMEM(rows, f32), pltpu.VMEM(row...  24.8 us
    pallas_call x1, Pallas kernels, local(): pl.pallas_call(kernel_b, out_shape=(jax.ShapeDtypeStruct(rows, f32),) * 2...  1.16 us

profile of v5, /device:TPU:1, one launch (start us, length us, event | category | flops | bytes accessed | tf_op | source)
XLA Modules:
  0.0 26.6 jit_solution(5376064526858480538)
XLA Ops:
  0.6 24.8 %shard_map.59 = (f32[24,64,128]{2,1,0:T(8,128)S(1)}, f32[24,64,128]{2,1,0:T(8,128)S(1)}) custom-call(f32[24,64,128]{2,1,0:T(8,128)} %bitcast.5, f32[24,64,128]{2,1,0:T(8,128)} %bitcast.6, f32[24,64,128]{2,1,0:T(8,128)} %bitcast.7, s32[64]{0:T(128)} %owner_hbm.1), custom_call_target="tpu_custom_call" | custom-call | tf_op jit(solution)/shard_map/pallas_call | solution.py:344
  25.5 1.2 %shard_map.60 = (f32[24,64,128]{2,1,0:T(8,128)}, f32[24,64,128]{2,1,0:T(8,128)}) custom-call(f32[24,64,128]{2,1,0:T(8,128)S(1)} %get-tuple-element.6.q1, f32[24,64,128]{2,1,0:T(8,128)S(1)} %get-tuple-element.7.q2), custom_call_target="tpu_custom_call" | custom-call | tf_op jit(solution)/shard_map/pallas_call | solution.py:368

commit v6 on v5

--- a/solution.py
+++ b/solution.py
@@ -16,7 +16,6 @@
 LAP = (-30.0 / 12.0, 16.0 / 12.0, -1.0 / 12.0)
 ALPHA = LAP[2] / DAMP[3]
 BETA = (LAP[1] - LAP[2] * DAMP[2] / DAMP[3]) / DAMP[3]
-P2_ORDER = (0, 1, 2, 3, 4, 7, 5, 6)
 REACH = 3
 
 
@@ -214,20 +213,18 @@
             fb[g] = jnp.concatenate(
                 [jnp.where(kind, above_g[h:h + 8], below_g[h:h + 8]) for h in (0, 8)], axis=0)
 
-    permute(P2_ORDER[0])
-    for n, plane in enumerate(P2_ORDER):
-        if n < 7:
-            permute(P2_ORDER[n + 1])
-
-        @pl.loop(0, 8)
-        def _(k):
-            peer = plane * 8 + k
-
-            @pl.when(peer != me)
-            def _():
-                pltpu.make_async_remote_copy(
-                    fb.at[peer, pl.ds(0, 10)], pair_rows(gb, my_slot), s_2, r_2.at[z],
-                    device_id={"gz": peer}, device_id_type=MESH).start()
+    def forward(peer):
+        @pl.when(peer != me)
+        def _():
+            pltpu.make_async_remote_copy(
+                fb.at[peer, pl.ds(0, 10)], pair_rows(gb, my_slot), s_2, r_2.at[z],
+                device_id={"gz": peer}, device_id_type=MESH).start()
+
+    for planes_now in ((0, 1, 2, 3), (4, 5, 6, 7)):
+        for plane in planes_now:
+            permute(plane)
+        for peer in sorted((p * 8 + k for p in planes_now for k in range(8)), key=lambda p: (9 * (p // 8) + (0, 16, 30, 30)[p % 8 // 2] + 10 * (p % 2), p)):
+            forward(peer)
 
     pltpu.make_async_copy(fb.at[me, pl.ds(0, 10)], pair_rows(gb, my_slot), r_2.at[z]).start()
 

time: 26.7 us -> 26 us (0.974)
  the two profiles are of different devices: /device:TPU:1 before, /device:TPU:2 now
where the time goes in v6:
time: 26 us; the launch traced here: 25.9 us
  Pallas kernels  25.3 us (97%)
  between operations  0.64 us (2%)
    pallas_call x1, Pallas kernels, local(): pl.pallas_call(kernel_a, out_shape=(pltpu.VMEM(rows, f32), pltpu.VMEM(row...  24.1 us
    pallas_call x1, Pallas kernels, local(): pl.pallas_call(kernel_b, out_shape=(jax.ShapeDtypeStruct(rows, f32),) * 2...  1.16 us

profile of v6, /device:TPU:2, one launch (start us, length us, event | category | flops | bytes accessed | tf_op | source)
XLA Modules:
  0.0 25.9 jit_solution(5735003159217512934)
XLA Ops:
  0.6 24.1 %shard_map.59 = (f32[24,64,128]{2,1,0:T(8,128)S(1)}, f32[24,64,128]{2,1,0:T(8,128)S(1)}) custom-call(f32[24,64,128]{2,1,0:T(8,128)} %bitcast.5, f32[24,64,128]{2,1,0:T(8,128)} %bitcast.6, f32[24,64,128]{2,1,0:T(8,128)} %bitcast.7, s32[64]{0:T(128)} %owner_hbm.1), custom_call_target="tpu_custom_call" | custom-call | tf_op jit(solution)/shard_map/pallas_call | solution.py:341
  24.8 1.2 %shard_map.60 = (f32[24,64,128]{2,1,0:T(8,128)}, f32[24,64,128]{2,1,0:T(8,128)}) custom-call(f32[24,64,128]{2,1,0:T(8,128)S(1)} %get-tuple-element.6.q1, f32[24,64,128]{2,1,0:T(8,128)S(1)} %get-tuple-element.7.q2), custom_call_target="tpu_custom_call" | custom-call | tf_op jit(solution)/shard_map/pallas_call | solution.py:365

commit v7 on v6

--- a/solution.py
+++ b/solution.py
@@ -70,8 +70,6 @@
         pl.semaphore_signal(barrier, inc=1, device_id={"gz": device(*d)}, device_id_type=MESH)
     pl.semaphore_signal(barrier, inc=1, device_id={"gy": 1 - gy}, device_id_type=MESH)
     pl.semaphore_signal(barrier, inc=1, device_id={"gx": 1 - gx}, device_id_type=MESH)
-    load_base.start()
-    load_accum.start()
 
     load_owner.wait()
     lanes = lane_iota()
@@ -134,7 +132,6 @@
 
     send_y = pltpu.make_async_remote_copy(
         xp.at[:, pl.ds(16, 64)], sy, s_y, r_y, device_id={"gy": 1 - gy}, device_id_type=MESH)
-    send_y.start()
     send_x = [
         pltpu.make_async_remote_copy(
             xp.at[:, pl.ds(16, 8)], xp.at[:, pl.ds(80, 8)], s_x.at[0], r_x.at[0],
@@ -147,6 +144,10 @@
     ]
     for s in send_x:
         s.start()
+    send_y.start()
+
+    load_base.start()
+    load_accum.start()
 
     pl.semaphore_wait(beside, 1)
     pl.semaphore_signal(beyond, inc=1, device_id={"gz": device(6, 3, 0)}, device_id_type=MESH)

time: 26 us -> 26 us (level)
  no operation moved by 1% of the time
where the time goes in v7:
time: 26 us; the launch traced here: 25.9 us
  Pallas kernels  25.3 us (97%)
  between operations  0.64 us (2%)
    pallas_call x1, Pallas kernels, local(): pl.pallas_call(kernel_a, out_shape=(pltpu.VMEM(rows, f32), pltpu.VMEM(row...  24.1 us
    pallas_call x1, Pallas kernels, local(): pl.pallas_call(kernel_b, out_shape=(jax.ShapeDtypeStruct(rows, f32),) * 2...  1.16 us

profile of v7, /device:TPU:2, one launch (start us, length us, event | category | flops | bytes accessed | tf_op | source)
XLA Modules:
  0.0 25.9 jit_solution(18040288093873594920)
XLA Ops:
  0.6 24.1 %shard_map.59 = (f32[24,64,128]{2,1,0:T(8,128)S(1)}, f32[24,64,128]{2,1,0:T(8,128)S(1)}) custom-call(f32[24,64,128]{2,1,0:T(8,128)} %bitcast.5, f32[24,64,128]{2,1,0:T(8,128)} %bitcast.6, f32[24,64,128]{2,1,0:T(8,128)} %bitcast.7, s32[64]{0:T(128)} %owner_hbm.1), custom_call_target="tpu_custom_call" | custom-call | tf_op jit(solution)/shard_map/pallas_call | solution.py:342
  24.8 1.2 %shard_map.60 = (f32[24,64,128]{2,1,0:T(8,128)}, f32[24,64,128]{2,1,0:T(8,128)}) custom-call(f32[24,64,128]{2,1,0:T(8,128)S(1)} %get-tuple-element.6.q1, f32[24,64,128]{2,1,0:T(8,128)S(1)} %get-tuple-element.7.q2), custom_call_target="tpu_custom_call" | custom-call | tf_op jit(solution)/shard_map/pallas_call | solution.py:366
